TPU v7x, 128 devices: a whole 4x4x4 slice. The times are simulated.
128 devices in a mesh: row: 8 (over x, core), col: 16 (over z, y).
Axes of the slice: x: 4, y: 4, z: 4, core: 2. Of those that a mesh axis runs over, the one named last changes fastest.
Arguments:
- kernel: bfloat16 [32768, 32768], P('row', 'col'), may hold values from -1 to 1
- random_cols: bfloat16 [32768, 256], P('row'), may hold values from -6 to 6
- tree_perm: int32 [32768], replicated, may hold values from 0 to 32767, as said below
- leaf_units: int32 [32], replicated, may hold values from 1 to 8, 160 in all
Outputs:
- bases: bfloat16 [4, 32768, 256], P(None, ('row', 'col'))
Inputs may be any that keep to these rules, and one draw needn't show every extreme that they name: `tree_perm`: A permutation. Cut tree positions and stored rows alike into blocks of 256 in order: every tree block takes at most 2 rows from any one stored block, some pair of blocks shares exactly 2, and every stored block gives 256 rows in all. `leaf_units`: they sum to 160.
All inputs are finite; a program needn't handle non-finite values.
Results may differ from a plain program's by a relative error of at most 0.0067.
Values may be sent and summed in bfloat16 or wider, within the bound.
No kernel may reach another device: no remote copies, remote signals or barrier semaphores. Data moves between devices by JAX's collectives and lax.ppermute only.
A program may use at most 192 MiB of HBM per device.

v0:
```python
import jax
import jax.numpy as jnp
from jax import lax
from jax.sharding import PartitionSpec as P

UNIT = 128
MINU = 4
LEVELS = 3


def shards(kernel, random_cols, tree_perm, leaf_units):
    width = random_cols.shape[1]
    partial_w = lax.dot_general(
        kernel, random_cols, (((0,), (0,)), ((), ())), preferred_element_type=jnp.float32
    )
    sample_w = lax.psum(partial_w, "row").astype(jnp.bfloat16)
    columns_count = lax.axis_size("col")
    rows_dev = kernel.shape[0] // columns_count
    sample = lax.psum_scatter(
        jnp.dot(kernel, sample_w, preferred_element_type=jnp.float32),
        "col",
        scatter_dimension=0,
        tiled=True,
    ).astype(jnp.bfloat16)
    total_rows = tree_perm.shape[0]
    device = lax.axis_index(("row", "col"))
    offset = device * rows_dev
    wanted = lax.dynamic_slice_in_dim(tree_perm, offset, rows_dev)
    inverse = (
        jnp.zeros((total_rows,), jnp.int32)
        .at[tree_perm]
        .set(jnp.arange(total_rows, dtype=jnp.int32))
    )
    placed = lax.dynamic_slice_in_dim(inverse, offset, rows_dev)
    everything = lax.all_gather(sample, ("row", "col"), axis=0, tiled=True)
    tree_rows = jnp.take(everything, wanted, axis=0)
    sizes = UNIT * (MINU - 1 + leaf_units)
    leaves = sizes.shape[0]
    ends = jnp.cumsum(sizes)
    positions = offset + jnp.arange(rows_dev, dtype=jnp.int32)
    leaf_of = jnp.sum(positions[:, None] >= ends[None, :], axis=1)
    reach = rows_dev // (UNIT * MINU) + 2
    offsets = jnp.arange(reach, dtype=jnp.int32)
    levels = LEVELS + 1
    node_ids = [leaf_of // 2**level for level in range(levels)]
    totals = []
    stored_leaf = jnp.sum(placed[:, None] >= ends[None, :], axis=1)
    leaf_range = jnp.arange(leaves, dtype=jnp.int32)
    chosen = stored_leaf[None, :] == leaf_range[:, None]
    masked = jnp.where(chosen[:, :, None], sample[None, :, :], jnp.zeros((), jnp.bfloat16))
    spread = jnp.einsum("lrs,rt->lst", masked, sample, preferred_element_type=jnp.float32)
    leaf_grams = lax.psum(spread, ("row", "col"))
    for level in range(levels):
        group = 2**level
        count = leaves // group
        node_grams = leaf_grams.reshape(count, group, width, width).sum(axis=1)
        index = jnp.minimum(node_ids[level][0] + offsets, count - 1)
        totals.append(jnp.take(node_grams, index, axis=0))
    identity_matrix = jnp.eye(width, dtype=jnp.float32)
    values = tree_rows.astype(jnp.float32).T
    results = []
    for level in range(levels):
        ids = node_ids[level]
        group = 2**level
        count = leaves // group
        node_sizes = sizes.reshape(count, group).sum(axis=1)
        candidate = ids[0] + offsets
        present = candidate <= ids[-1]
        counts = jnp.take(node_sizes, jnp.minimum(candidate, count - 1)).astype(jnp.float32)
        mean = jnp.where(
            present[:, None, None], totals[level] / counts[:, None, None], identity_matrix[None]
        )
        factor = jnp.linalg.cholesky(mean)
        basis = jnp.zeros((rows_dev, width), jnp.float32)
        for which in range(reach):
            solved = jax.scipy.linalg.solve_triangular(factor[which], values, lower=True).T
            basis = basis + jnp.where((ids == candidate[which])[:, None], solved, 0.0)
        results.append(basis.astype(jnp.bfloat16))
    return jnp.stack(results)


def solution(mesh):
    return jax.shard_map(
        shards,
        mesh=mesh,
        in_specs=(P("row", "col"), P("row", None), P(), P()),
        out_specs=P(None, ("row", "col"), None),
        check_vma=False,
    )
```

profile of v0, /device:TPU:1, one launch (start us, length us, event | category | flops | bytes accessed | tf_op | source)
XLA Modules:
  0.0 931.9 jit_solution(916774655061557949)
XLA Ops:
  17.8 52.9 %all-reduce.5 = bf16[2048,256]{1,0:T(8,128)(2,1)S(1)} all-reduce(f32[2048,256]{1,0:T(8,128)} %fusion.100), channel_id=1, replica_groups=mesh['row'=8,'col'=16] {'row'}, use_global_device_ids=true, to_apply=%region_4.5 | all-reduce | flops 524288 | bytes 3145728 | tf_op jit(solution)/shard_map/psum | solution.py:16
  81.9 120.1 %scatter_custom_fusion = s32[32768]{0:T(1024)S(1)} fusion(s32[32768]{0:T(1024)S(1)} %compare_select_fusion, s32[32768]{0:T(1024)S(1)} %iota.117, s32[]{:T(128)} %copy.139), kind=kCustom, calls=%fused_computation.181 | custom fusion | bytes 131076 | tf_op jit(solution)/shard_map/scatter | solution.py:32
  253.2 119.0 %all-reduce.4.cloned.1.call-done = f32[32,256,256]{2,1,0:T(8,128)} async-done(((f32[32,256,256]{2,1,0:T(8,128)}), f32[32,256,256]{2,1,0:T(8,128)}) %all-reduce.4.cloned.1.call-update) | async-done | bytes 8388624 | tf_op jit(solution)/shard_map/psum | solution.py:52
  400.0 23.5 %custom-call.29 = f32[2,128,128]{2,1,0:T(8,128)S(1)} custom-call(f32[2,128,128]{2,1,0:T(8,128)S(1)} %cholesky.350), custom_call_target="Cholesky" | custom-call | tf_op jit(solution)/shard_map/jit(cholesky)/cholesky | solution.py:73
  423.7 23.5 %custom-call.39 = f32[2,128,128]{2,1,0:T(8,128)S(1)} custom-call(f32[2,128,128]{2,1,0:T(8,128)S(1)} %cholesky.356), custom_call_target="Cholesky" | custom-call | tf_op jit(solution)/shard_map/jit(cholesky)/cholesky | solution.py:73
  448.3 23.5 %custom-call.34 = f32[2,128,128]{2,1,0:T(8,128)S(1)} custom-call(f32[2,128,128]{2,1,0:T(8,128)S(1)} %cholesky.353), custom_call_target="Cholesky" | custom-call | tf_op jit(solution)/shard_map/jit(cholesky)/cholesky | solution.py:73
  472.1 23.9 %custom-call.44 = f32[2,128,128]{2,1,0:T(8,128)S(1)} custom-call(f32[2,128,128]{2,1,0:T(8,128)S(1)} %cholesky.359), custom_call_target="Cholesky" | custom-call | tf_op jit(solution)/shard_map/jit(cholesky)/cholesky | solution.py:73
  497.4 19.7 %custom-call.30 = f32[2,1,128,128]{2,3,1,0:T(8,128)S(1)} custom-call(f32[2,1,128,128]{3,2,1,0:T(8,128)S(1)} %get-tuple-element.180), custom_call_target="InvertDiagBlocksLowerTriangular" | custom-call | tf_op jit(solution)/shard_map/jit(cholesky)/cholesky | solution.py:73
  517.8 23.5 %custom-call.31 = f32[2,128,128]{2,1,0:T(8,128)S(1)} custom-call(f32[2,128,128]{2,1,0:T(8,128)S(1)} %convolution_subtract_fusion.11), custom_call_target="Cholesky" | custom-call | tf_op jit(solution)/shard_map/jit(cholesky)/cholesky | solution.py:73
  541.3 19.8 %custom-call.35 = f32[2,1,128,128]{2,3,1,0:T(8,128)S(1)} custom-call(f32[2,1,128,128]{3,2,1,0:T(8,128)S(1)} %get-tuple-element.178), custom_call_target="InvertDiagBlocksLowerTriangular" | custom-call | tf_op jit(solution)/shard_map/jit(cholesky)/cholesky | solution.py:73
  563.7 23.5 %custom-call.36 = f32[2,128,128]{2,1,0:T(8,128)S(1)} custom-call(f32[2,128,128]{2,1,0:T(8,128)S(1)} %convolution_subtract_fusion.10), custom_call_target="Cholesky" | custom-call | tf_op jit(solution)/shard_map/jit(cholesky)/cholesky | solution.py:73
  587.2 21.1 %custom-call.40 = f32[2,1,128,128]{2,3,1,0:T(8,128)} custom-call(f32[2,1,128,128]{3,2,1,0:T(8,128)} %get-tuple-element.177), custom_call_target="InvertDiagBlocksLowerTriangular" | custom-call | tf_op jit(solution)/shard_map/jit(cholesky)/cholesky | solution.py:73
  610.5 25.1 %custom-call.41 = f32[2,128,128]{2,1,0:T(8,128)} custom-call(f32[2,128,128]{2,1,0:T(8,128)} %convolution_subtract_fusion.9), custom_call_target="Cholesky" | custom-call | tf_op jit(solution)/shard_map/jit(cholesky)/cholesky | solution.py:73
  636.5 21.1 %custom-call.45 = f32[2,1,128,128]{2,3,1,0:T(8,128)} custom-call(f32[2,1,128,128]{3,2,1,0:T(8,128)} %get-tuple-element.179), custom_call_target="InvertDiagBlocksLowerTriangular" | custom-call | tf_op jit(solution)/shard_map/jit(cholesky)/cholesky | solution.py:73
  659.9 24.3 %custom-call.46 = f32[2,128,128]{2,1,0:T(8,128)S(1)} custom-call(f32[2,128,128]{2,1,0:T(8,128)} %convolution_subtract_fusion.8), custom_call_target="Cholesky" | custom-call | tf_op jit(solution)/shard_map/jit(cholesky)/cholesky | solution.py:73
  692.3 20.1 %custom-call.48 = f32[2,128,128]{1,2,0:T(8,128)S(1)} custom-call(f32[2,128,128]{2,1,0:T(8,128)S(1)} %get-tuple-element.64), custom_call_target="InvertDiagBlocksLowerTriangular" | custom-call | tf_op jit(solution)/shard_map/jit(_solve_triangular)/triangular_solve | solution.py:76
  716.4 20.3 %custom-call.47 = f32[2,128,128]{1,2,0:T(8,128)} custom-call(f32[2,128,128]{2,1,0:T(8,128)S(1)} %get-tuple-element.63), custom_call_target="InvertDiagBlocksLowerTriangular" | custom-call | tf_op jit(solution)/shard_map/jit(_solve_triangular)/triangular_solve | solution.py:76
  740.8 19.7 %custom-call.43 = f32[2,128,128]{1,2,0:T(8,128)S(1)} custom-call(f32[2,128,128]{2,1,0:T(8,128)S(1)} %get-tuple-element.62), custom_call_target="InvertDiagBlocksLowerTriangular" | custom-call | tf_op jit(solution)/shard_map/jit(_solve_triangular)/triangular_solve | solution.py:76
  764.5 19.7 %custom-call.42 = f32[2,128,128]{1,2,0:T(8,128)S(1)} custom-call(f32[2,128,128]{2,1,0:T(8,128)S(1)} %get-tuple-element.61), custom_call_target="InvertDiagBlocksLowerTriangular" | custom-call | tf_op jit(solution)/shard_map/jit(_solve_triangular)/triangular_solve | solution.py:76
  788.1 19.7 %custom-call.38 = f32[2,128,128]{1,2,0:T(8,128)S(1)} custom-call(f32[2,128,128]{2,1,0:T(8,128)S(1)} %get-tuple-element.60), custom_call_target="InvertDiagBlocksLowerTriangular" | custom-call | tf_op jit(solution)/shard_map/jit(_solve_triangular)/triangular_solve | solution.py:76
  811.7 20.5 %custom-call.37 = f32[2,128,128]{1,2,0:T(8,128)} custom-call(f32[2,128,128]{2,1,0:T(8,128)S(1)} %get-tuple-element.59), custom_call_target="InvertDiagBlocksLowerTriangular" | custom-call | tf_op jit(solution)/shard_map/jit(_solve_triangular)/triangular_solve | solution.py:76
  836.1 20.3 %custom-call.33 = f32[2,128,128]{1,2,0:T(8,128)} custom-call(f32[2,128,128]{2,1,0:T(8,128)S(1)} %get-tuple-element.58), custom_call_target="InvertDiagBlocksLowerTriangular" | custom-call | tf_op jit(solution)/shard_map/jit(_solve_triangular)/triangular_solve | solution.py:76
  860.0 20.3 %custom-call.32 = f32[2,128,128]{1,2,0:T(8,128)} custom-call(f32[2,128,128]{2,1,0:T(8,128)S(1)} %get-tuple-element.57), custom_call_target="InvertDiagBlocksLowerTriangular" | custom-call | tf_op jit(solution)/shard_map/jit(_solve_triangular)/triangular_solve | solution.py:76
  880.3 22.6 %copy.47 = bf16[32768,256]{1,0:T(8,128)(2,1)} copy(bf16[32768,256]{0,1:T(8,128)(2,1)} %all-gather.2.cloned.1.call-done) | data formatting | bytes 33554432 | tf_op jit(solution)/shard_map/all_gather | solution.py:35
  (274 shorter events, 200.8 us)
Async XLA Ops:
  6.5 1.6 copy-start
  6.5 195.6 %reduce-scatter.2.cloned.1.call-start = ((), (), s32[]{:S(2)}) async-start(), calls=%async_computation.1 | async-start | bytes 4456448 | tf_op jit(solution)/shard_map/reduce_scatter | solution.py:19
  80.9 291.2 %all-reduce.4.cloned.1.call-start = ((), (), s32[]{:S(2)}) async-start(), calls=%async_computation.2 | async-start | bytes 16777216 | tf_op jit(solution)/shard_map/psum | solution.py:52
  203.1 4.5 copy-start.2
  207.7 672.6 %all-gather.2.cloned.1.call-start = ((), (), s32[]{:S(2)}) async-start(), calls=%async_computation.3 | async-start | bytes 16908288 | tf_op jit(solution)/shard_map/all_gather | solution.py:35
  423.7 93.4 %copy-start.7 = (f32[2,256,256]{2,1,0:T(8,128)S(1)}, f32[2,256,256]{2,1,0:T(8,128)}, u32[]{:S(2)}) copy-start(f32[2,256,256]{2,1,0:T(8,128)} %copy-done.6) | copy-start | bytes 1572868
  495.9 1.5 copy-start.9
  517.8 166.3 %copy-start.10 = (f32[2,128,128]{2,1,0:T(8,128)S(1)}, f32[2,128,128]{2,1,0:T(8,128)}, u32[]{:S(2)}) copy-start(f32[2,128,128]{2,1,0:T(8,128)} %copy-done.9) | copy-start | bytes 393220
  685.1 1.0 copy-start.3
  807.8 108.1 %copy-start.13 = (f32[2,128,128]{1,2,0:T(8,128)}, f32[2,128,128]{1,2,0:T(8,128)S(1)}, u32[]{:S(2)}) copy-start(f32[2,128,128]{1,2,0:T(8,128)S(1)} %custom-call.38) | copy-start | bytes 393220
  836.1 66.9 %copy-start.5 = (f32[256,256]{1,0:T(8,128)}, f32[256,256]{1,0:T(8,128)S(1)}, u32[]{:S(2)}) copy-start(f32[256,256]{1,0:T(8,128)S(1)} %get-tuple-element.602) | copy-start | bytes 786436
  880.3 31.8 %copy-start.24 = (pred[256]{0:T(512)(128)(4,1)S(1)}, pred[256]{0:T(512)(128)(4,1)}, u32[]{:S(2)}) copy-start(pred[256]{0:T(512)(128)(4,1)} %get-tuple-element.139) | copy-start | bytes 772
  880.3 32.8 %copy-start.12 = (f32[2,128,128]{1,2,0:T(8,128)S(1)}, f32[2,128,128]{1,2,0:T(8,128)}, u32[]{:S(2)}) copy-start(f32[2,128,128]{1,2,0:T(8,128)} %custom-call.47) | copy-start | bytes 393220
  912.1 10.5 %copy-start.14 = (f32[2,128,128]{1,2,0:T(8,128)S(1)}, f32[2,128,128]{1,2,0:T(8,128)}, u32[]{:S(2)}) copy-start(f32[2,128,128]{1,2,0:T(8,128)} %custom-call.33) | copy-start | bytes 393220
  912.1 10.8 %copy-start.15 = (f32[2,128,128]{1,2,0:T(8,128)S(1)}, f32[2,128,128]{1,2,0:T(8,128)}, u32[]{:S(2)}) copy-start(f32[2,128,128]{1,2,0:T(8,128)} %custom-call.32) | copy-start | bytes 393220
  912.4 11.4 %copy-start.18 = (pred[256]{0:T(512)(128)(4,1)S(1)}, pred[256]{0:T(512)(128)(4,1)}, u32[]{:S(2)}) copy-start(pred[256]{0:T(512)(128)(4,1)} %get-tuple-element.187) | copy-start | bytes 772
  912.5 11.4 %copy-start.19 = (pred[256]{0:T(512)(128)(4,1)S(1)}, pred[256]{0:T(512)(128)(4,1)}, u32[]{:S(2)}) copy-start(pred[256]{0:T(512)(128)(4,1)} %get-tuple-element.188) | copy-start | bytes 772
  913.1 10.8 %copy-start.16 = (pred[256]{0:T(512)(128)(4,1)S(1)}, pred[256]{0:T(512)(128)(4,1)}, u32[]{:S(2)}) copy-start(pred[256]{0:T(512)(128)(4,1)} %get-tuple-element.226) | copy-start | bytes 772
  913.1 10.8 %copy-start.17 = (pred[256]{0:T(512)(128)(4,1)S(1)}, pred[256]{0:T(512)(128)(4,1)}, u32[]{:S(2)}) copy-start(pred[256]{0:T(512)(128)(4,1)} %get-tuple-element.227) | copy-start | bytes 772
  913.7 10.3 %copy-start.22 = (pred[256]{0:T(512)(128)(4,1)S(1)}, pred[256]{0:T(512)(128)(4,1)}, u32[]{:S(2)}) copy-start(pred[256]{0:T(512)(128)(4,1)} %get-tuple-element.183) | copy-start | bytes 772
  913.7 10.3 %copy-start.23 = (pred[256]{0:T(512)(128)(4,1)S(1)}, pred[256]{0:T(512)(128)(4,1)}, u32[]{:S(2)}) copy-start(pred[256]{0:T(512)(128)(4,1)} %get-tuple-element.184) | copy-start | bytes 772
  914.3 9.7 %copy-start.20 = (pred[256]{0:T(512)(128)(4,1)S(1)}, pred[256]{0:T(512)(128)(4,1)}, u32[]{:S(2)}) copy-start(pred[256]{0:T(512)(128)(4,1)} %get-tuple-element.181) | copy-start | bytes 772
  914.3 9.7 %copy-start.21 = (pred[256]{0:T(512)(128)(4,1)S(1)}, pred[256]{0:T(512)(128)(4,1)}, u32[]{:S(2)}) copy-start(pred[256]{0:T(512)(128)(4,1)} %get-tuple-element.182) | copy-start | bytes 772
  916.2 9.0 copy-start.1
  (5 other events, 4.2 us)
Sparse Core Ops, SparseCore 0:
  81.0 79.6 reduce-scatter.1
  207.8 164.3 all-reduce.3
  375.0 98.1 all-gather.1
where the time goes:
time: 940 us; the launch traced here: 932 us
  other arithmetic  481 us (51%)
  local copies, waits for them, and re-layouts  208 us (22%)
  waiting for transfers between devices  119 us (13%)
  blocking collectives  52.9 us (6%)
  matrix products  43.3 us (5%)
  between operations  14.6 us (2%)
  starting transfers between devices  12 us (1%)
    another operation x28, other arithmetic, shards(): factor = jnp.linalg.cholesky(mean)  276 us
    another operation x14, other arithmetic, shards(): jax.scipy.linalg.solve_triangular(factor[which], values, lower=True)  162 us
    scatter x1, local copies, waits for them, and re-layouts, shards(): inverse = jnp.zeros((total_rows,), jnp.int32).at[tree_perm].set(jnp.arang...  120 us
    psum x1, waiting for transfers between devices, shards(): leaf_grams = lax.psum(spread, ('row', 'col'))  119 us
    psum x1, blocking collectives, shards(): sample_w = lax.psum(partial_w, 'row').astype(jnp.bfloat16)  52.9 us
    another operation x49, local copies, waits for them, and re-layouts, shards(): jax.scipy.linalg.solve_triangular(factor[which], values, lower=True)  31.3 us
    all_gather x1, local copies, waits for them, and re-layouts, shards(): everything = lax.all_gather(sample, ('row', 'col'), axis=0, tiled=True)  22.6 us
  transfers between devices with their start and end apart: 3, of which 1 were waited for; matrix products, arithmetic and copies ran while one was open for 71% of the time, Pallas kernels for 0%

commit v1 on v0

v1 whole, which is shorter than its diff:
```python
import functools

import jax
import jax.numpy as jnp
from jax import lax
from jax.experimental import pallas as pl
from jax.experimental.pallas import tpu as pltpu
from jax.sharding import PartitionSpec as P

UNIT = 128
MINU = 4
LEVELS = 3
BOTH = ("row", "col")
HIGHEST = lax.Precision.HIGHEST


def iota(shape, dim):
    return lax.broadcasted_iota(jnp.int32, shape, dim)


def second_pass(first_ref, kernel_ref, w_ref, tree_ref, out_ref, spread_ref):
    step = pl.program_id(0)
    panel = pl.num_programs(0)
    partial = jnp.dot(
        kernel_ref[...], w_ref[...], preferred_element_type=jnp.float32
    ).astype(jnp.bfloat16)
    tree = tree_ref[...]
    blocks, rows = tree.shape
    here = lax.shift_right_logical(tree, 8) == first_ref[0] + step
    inner = lax.bitwise_and(tree, rows - 1)
    low = jnp.min(jnp.where(here, inner, rows), axis=1, keepdims=True)
    high = jnp.max(jnp.where(here, inner, -1), axis=1, keepdims=True)
    lanes = iota((blocks, rows), 1)
    for which, chosen in enumerate((low, high)):
        pick = (lanes == chosen).astype(jnp.float32).astype(jnp.bfloat16)
        moved = jnp.dot(pick, partial, preferred_element_type=jnp.float32)
        width = moved.shape[1]
        for half in range(width // 128):
            column = which * (width // 128) + half
            spread_ref[column, pl.ds(step, blocks, stride=panel), :] = moved[
                :, half * 128 : (half + 1) * 128
            ]

    @pl.when(step == panel - 1)
    def _():
        for column in range(spread_ref.shape[0]):
            out_ref[:, column * 128 : (column + 1) * 128] = spread_ref[column].astype(
                jnp.bfloat16
            )


def collect(wanted_ref, parts_ref, rows_ref, gram_ref):
    row_devices, col_devices, inner, wide = parts_ref.shape
    blocks = row_devices * inner
    width = wide // 2
    groups = []
    for row in range(row_devices):
        total = parts_ref[row, 0].astype(jnp.float32)
        for col in range(1, col_devices):
            total = total + parts_ref[row, col].astype(jnp.float32)
        groups.append(total.astype(jnp.bfloat16))
    sample = jnp.concatenate(groups, axis=0)
    wanted = wanted_ref[...]
    rows = wanted.shape[0]
    block = lax.shift_right_logical(wanted, 8)
    inside = lax.bitwise_and(wanted, rows - 1)
    same = block == iota((rows, blocks), 1)
    low = jnp.min(jnp.where(same, inside, rows), axis=0, keepdims=True)
    high = jnp.max(jnp.where(same, inside, -1), axis=0, keepdims=True)
    ordered = jnp.zeros((rows, width), jnp.float32)
    for which, chosen in enumerate((low, high)):
        pick = jnp.where(same & (inside == chosen), 1.0, 0.0).astype(jnp.bfloat16)
        ordered = ordered + jnp.dot(
            pick,
            sample[:, which * width : (which + 1) * width],
            preferred_element_type=jnp.float32,
        )
    ordered = ordered.astype(jnp.bfloat16)
    rows_ref[...] = ordered
    half = width // 2
    for unit in range(rows // UNIT):
        piece = ordered[unit * UNIT : (unit + 1) * UNIT]
        left, right = piece[:, :half], piece[:, half:]
        pairs = ((left, left), (right, left), (right, right))
        for index, (one, two) in enumerate(pairs):
            gram = lax.dot_general(
                one, two, (((0,), (0,)), ((), ())), preferred_element_type=jnp.float32
            )
            gram_ref[pl.ds(unit * 4 + index, half, stride=8), :] = gram
        gram_ref[pl.ds(unit * 4 + 3, half, stride=8), :] = jnp.zeros(
            (half, half), jnp.float32
        )


def leaf_of_unit(units_ref, unit):
    leaf = jnp.zeros_like(unit)
    end = jnp.int32(0)
    for index in range(units_ref.shape[0]):
        end = end + units_ref[index] + (MINU - 1)
        leaf = leaf + (unit >= end).astype(jnp.int32)
    return leaf


def node_sums(units_ref, parts_ref, out_ref):
    devices = out_ref.shape[0]
    units = 2 * devices
    slots = 2 * (LEVELS + 1)
    unit_leaf = leaf_of_unit(units_ref, iota((8, units), 1))[0:1]
    row = iota((devices * slots, 128), 0)
    slot = lax.bitwise_and(row, slots - 1)
    level = lax.shift_right_logical(slot, 1)
    own = 2 * lax.shift_right_logical(row, 3) + lax.bitwise_and(slot, 1)
    own_node = lax.shift_right_logical(leaf_of_unit(units_ref, own), level)
    member = []
    for part in range(units // 128):
        leaf = jnp.broadcast_to(unit_leaf[:, part * 128 : (part + 1) * 128], row.shape)
        match = lax.shift_right_logical(leaf, level) == own_node
        member.append(jnp.where(match, 1.0, 0.0).astype(jnp.bfloat16))
    member = jnp.concatenate(member, axis=1)
    for index in range(3):
        left = parts_ref[pl.ds(index, units, stride=4), :]
        total = jnp.zeros((devices * slots, left.shape[1]), jnp.float32)
        for _ in range(3):
            piece = left.astype(jnp.bfloat16)
            left = left - piece.astype(jnp.float32)
            total = total + jnp.dot(member, piece, preferred_element_type=jnp.float32)
        out_ref[:, index * slots : (index + 1) * slots, :] = total.reshape(
            devices, slots, total.shape[1]
        )


def spread_lane(values, lane):
    return jnp.take_along_axis(values, jnp.full(values.shape, lane, jnp.int32), axis=1)


def invert_factors(work_ref, solved_ref):
    count, size, lanes = work_ref.shape
    lane = iota((8, lanes), 1)
    sub = iota((8, lanes), 0)
    chunk = 4

    def block_step(block, carry):
        base = pl.multiple_of(block * 8, 8)
        inside = (lane >= base) & (lane < base + 8)
        eye = lane - base == sub
        for which in range(count):
            rows = work_ref[which, pl.ds(base, 8), :]
            columns = [spread_lane(rows, base + i) for i in range(8)]
            value = jnp.where(inside, jnp.where(eye, 1.0, 0.0), rows)
            scales = []
            for i in range(8):
                pivot = jnp.broadcast_to(columns[i][i : i + 1], sub.shape)
                scale = lax.rsqrt(pivot)
                scales.append(scale)
                below = jnp.where(sub > i, columns[i] * scale, 0.0)
                keep = jnp.where(sub == i, scale, 1.0)
                for k in range(i, 8):
                    top = jnp.broadcast_to(columns[k][i : i + 1], sub.shape) * scale
                    columns[k] = columns[k] * keep - below * top
                top = jnp.broadcast_to(value[i : i + 1], sub.shape) * scale
                value = value * keep - below * top
            work_ref[which, pl.ds(base, 8), :] = jnp.where(lane <= base + sub, value, 0.0)
            for i in reversed(range(8)):
                top = jnp.broadcast_to(value[i : i + 1], sub.shape) * scales[i]
                above = jnp.where(sub < i, columns[i], 0.0)
                value = jnp.where(sub == i, top, value) - above * top
            solved_ref[which] = value

        def update(group, carry):
            for inner in range(chunk):
                index = group * chunk + inner
                start = pl.multiple_of(index * 8, 8)
                later = jnp.full(sub.shape, index, jnp.int32) > block
                for which in range(count):
                    rows = work_ref[which, pl.ds(start, 8), :]
                    total = jnp.where(inside, 0.0, rows)
                    for i in range(8):
                        row = jnp.broadcast_to(solved_ref[which, i : i + 1, :], sub.shape)
                        total = total - spread_lane(rows, base + i) * row
                    work_ref[which, pl.ds(start, 8), :] = jnp.where(later, total, rows)
            return carry

        return lax.fori_loop((block + 1) // chunk, size // 8 // chunk, update, carry)

    lax.fori_loop(0, size // 8, block_step, 0)


def dot_t(one, two, precision=HIGHEST):
    return lax.dot_general(
        one,
        two,
        (((1,), (1,)), ((), ())),
        precision=precision,
        preferred_element_type=jnp.float32,
    )


def node_bases(
    device_ref, units_ref, node_ref, rows_ref, out_ref, work_ref, side_ref, last_ref, solved_ref
):
    slots = work_ref.shape[0]
    half = work_ref.shape[1]
    stride = 3 * slots
    scales = []
    for slot in range(slots):
        level, unit = slot // 2, 2 * device_ref[0] + slot % 2
        leaf = jnp.int32(0)
        end = jnp.int32(0)
        for index in range(units_ref.shape[0]):
            end = end + units_ref[index] + (MINU - 1)
            leaf = leaf + (unit >= end).astype(jnp.int32)
        node = lax.shift_right_logical(leaf, level)
        count = jnp.int32(0)
        for index in range(units_ref.shape[0]):
            size = units_ref[index] + (MINU - 1)
            count = count + jnp.where(node == index >> level, size, 0)
        size = jnp.full((half, half), count * UNIT, jnp.int32).astype(jnp.float32)
        scales.append(size)
    for slot in range(slots):
        work_ref[slot] = node_ref[pl.ds(slot, half, stride=stride), :] / scales[slot]
    invert_factors(work_ref, solved_ref)
    for slot in range(slots):
        below = node_ref[pl.ds(slots + slot, half, stride=stride), :] / scales[slot]
        side = dot_t(below, work_ref[slot])
        side_ref[slot] = side
        corner = node_ref[pl.ds(2 * slots + slot, half, stride=stride), :] / scales[slot]
        last_ref[slot] = corner - dot_t(side, side)
    invert_factors(last_ref, solved_ref)
    for slot in range(slots):
        level, unit = slot // 2, slot % 2
        piece = rows_ref[unit * UNIT : (unit + 1) * UNIT, :].astype(jnp.float32)
        first = dot_t(piece[:, :half], work_ref[slot])
        rest = piece[:, half:] - dot_t(first, side_ref[slot])
        second = dot_t(rest, last_ref[slot])
        place = slice(unit * UNIT, (unit + 1) * UNIT)
        out_ref[level, place, :half] = first.astype(jnp.bfloat16)
        out_ref[level, place, half:] = second.astype(jnp.bfloat16)


def shards(kernel, random_cols, tree_perm, leaf_units):
    f32, bf16 = jnp.float32, jnp.bfloat16
    width = random_cols.shape[1]
    half = width // 2
    row_devices, col_devices = lax.axis_size("row"), lax.axis_size("col")
    devices = row_devices * col_devices
    total_rows = tree_perm.shape[0]
    rows_dev = total_rows // devices
    panel = kernel.shape[0] // rows_dev
    slots = 2 * (LEVELS + 1)
    row = lax.axis_index("row")
    device = row * col_devices + lax.axis_index("col")
    vmem = pl.BlockSpec(memory_space=pltpu.VMEM)
    smem = pl.BlockSpec(memory_space=pltpu.SMEM)

    def exchange(values, axes):
        return lax.all_to_all(values, axes, 0, 0, tiled=True)

    partial_w = lax.dot_general(
        kernel, random_cols, (((0,), (0,)), ((), ())), preferred_element_type=f32
    ).astype(bf16)
    chunk = kernel.shape[1] // row_devices
    arrived = exchange(partial_w.reshape(row_devices, chunk, width), "row")
    own_w = jnp.sum(arrived.astype(f32), axis=0).astype(bf16)
    sample_w = exchange(jnp.broadcast_to(own_w[None], (row_devices, chunk, width)), "row")
    sample_w = sample_w.reshape(kernel.shape[1], width)

    tree = tree_perm.reshape(devices, rows_dev)
    parts = pl.pallas_call(
        second_pass,
        grid_spec=pltpu.PrefetchScalarGridSpec(
            num_scalar_prefetch=1,
            grid=(panel,),
            in_specs=[
                pl.BlockSpec((rows_dev, kernel.shape[1]), lambda s, first: (s, 0)),
                pl.BlockSpec((kernel.shape[1], width), lambda s, first: (0, 0)),
                pl.BlockSpec((devices, rows_dev), lambda s, first: (0, 0)),
            ],
            out_specs=pl.BlockSpec((devices * panel, 2 * width), lambda s, first: (0, 0)),
            scratch_shapes=[pltpu.VMEM((4, devices * panel, 128), f32)],
        ),
        out_shape=jax.ShapeDtypeStruct((devices * panel, 2 * width), bf16),
        name="second_pass",
    )((row * panel)[None], kernel, sample_w, tree)
    parts = exchange(parts.reshape(devices, panel, 2 * width), BOTH)

    wanted = lax.dynamic_slice_in_dim(tree_perm, device * rows_dev, rows_dev)
    wanted = jnp.broadcast_to(wanted[:, None], (rows_dev, devices))
    tree_rows, grams = pl.pallas_call(
        collect,
        in_specs=[vmem, vmem],
        out_specs=[vmem, vmem],
        out_shape=[
            jax.ShapeDtypeStruct((rows_dev, width), bf16),
            jax.ShapeDtypeStruct((devices * 8, half), f32),
        ],
        name="collect",
    )(wanted, parts.reshape(row_devices, col_devices, panel, 2 * width))

    grams = exchange(grams.reshape(devices, 8, half), BOTH)
    nodes = pl.pallas_call(
        node_sums,
        in_specs=[smem, vmem],
        out_specs=vmem,
        out_shape=jax.ShapeDtypeStruct((devices, 3 * slots, half), f32),
        name="node_sums",
    )(leaf_units, grams.reshape(devices * 8, half))
    nodes = exchange(nodes, BOTH)

    return pl.pallas_call(
        node_bases,
        in_specs=[smem, smem, vmem, vmem],
        out_specs=vmem,
        out_shape=jax.ShapeDtypeStruct((LEVELS + 1, rows_dev, width), bf16),
        scratch_shapes=[pltpu.VMEM((slots, half, half), f32)] * 3
        + [pltpu.VMEM((slots, 8, half), f32)],
        name="node_bases",
    )(device[None], leaf_units, nodes.reshape(devices * 3 * slots, half), tree_rows)


def solution(mesh):
    return jax.shard_map(
        shards,
        mesh=mesh,
        in_specs=(P("row", "col"), P("row", None), P(), P()),
        out_specs=P(None, ("row", "col"), None),
        check_vma=False,
    )
```

time: 940 us -> 247 us (0.26)
  other arithmetic: 481 us -> 0.15 us
  local copies, waits for them, and re-layouts: 208 us -> 5.13 us
  Pallas kernels: 0 us -> 106 us
  waiting for transfers between devices: 119 us -> 43.1 us
  matrix products: 43.3 us -> 8.46 us
  blocking collectives: 52.9 us -> 69.7 us
  between operations: 14.6 us -> 0.04 us
    another operation x49 -> x0, other arithmetic: 438 us -> none  [the longest x28 276 us: shards(): factor = jnp.linalg.cholesky(mean)]
    scatter x1 -> x0, local copies, waits for them, and re-layouts: 120 us -> none  [shards(): inverse = jnp.zeros((total_rows,), jnp.int32).at[tree_perm].set(jnp.arang...]
    psum x1 -> x0, waiting for transfers between devices: 119 us -> none  [shards(): leaf_grams = lax.psum(spread, ('row', 'col'))]
    pallas_call x0 -> x4, Pallas kernels: none -> 106 us  [the longest x1 78.3 us: shards(): pl.pallas_call(node_bases, in_specs=[smem, smem, vmem, vmem], out_specs=v...]
    all_to_all x0 -> x3, blocking collectives: none -> 69.7 us  [exchange(): return lax.all_to_all(values, axes, 0, 0, tiled=True)]
    psum x1 -> x0, blocking collectives: 52.9 us -> none  [shards(): sample_w = lax.psum(partial_w, 'row').astype(jnp.bfloat16)]
    all_to_all x0 -> x2, waiting for transfers between devices: none -> 43.1 us  [exchange(): return lax.all_to_all(values, axes, 0, 0, tiled=True)]
    another operation x67 -> x0, local copies, waits for them, and re-layouts: 33.6 us -> none  [the longest x49 31.3 us: shards(): jax.scipy.linalg.solve_triangular(factor[which], values, lower=True)]
  transfers between devices with their start and end apart: 3 -> 2, of which waited for: 1 -> 2; matrix products, arithmetic and copies ran while one was open for 71% -> 0% of each run, Pallas kernels for 0% -> 0%
where the time goes in v1:
time: 247 us; the launch traced here: 246 us
  Pallas kernels  106 us (43%)
  blocking collectives  69.7 us (28%)
  waiting for transfers between devices  43.1 us (17%)
  starting transfers between devices  14 us (6%)
  matrix products  8.46 us (3%)
  local copies, waits for them, and re-layouts  5.13 us (2%)
    pallas_call x1, Pallas kernels, shards(): pl.pallas_call(node_bases, in_specs=[smem, smem, vmem, vmem], out_specs=v...  78.3 us
    all_to_all x3, blocking collectives, exchange(): return lax.all_to_all(values, axes, 0, 0, tiled=True)  69.7 us
    all_to_all x2, waiting for transfers between devices, exchange(): return lax.all_to_all(values, axes, 0, 0, tiled=True)  43.1 us
    pallas_call x1, Pallas kernels, shards(): pl.pallas_call(second_pass, grid_spec=pltpu.PrefetchScalarGridSpec(num_sc...  18.9 us
    all_to_all x2, starting transfers between devices, exchange(): return lax.all_to_all(values, axes, 0, 0, tiled=True)  14 us
    dot_general x1, matrix products, shards(): lax.dot_general(kernel, random_cols, (((0,), (0,)), ((), ())), preferred_...  8.46 us
    pallas_call x1, Pallas kernels, shards(): pl.pallas_call(node_sums, in_specs=[smem, vmem], out_specs=vmem, out_shap...  5.26 us
  transfers between devices with their start and end apart: 2, of which 2 were waited for; matrix products, arithmetic and copies ran while one was open for 0% of the time, Pallas kernels for 0%

profile of v1, /device:TPU:1, one launch (start us, length us, event | category | flops | bytes accessed | tf_op | source)
XLA Modules:
  0.0 246.4 jit_solution(17006321519322632790)
XLA Ops:
  0.0 0.0 copy-start
  0.0 1.6 copy-done
  1.6 8.5 %convolution_convert_fusion = bf16[2048,256]{1,0:T(8,128)(2,1)S(1)} fusion(bf16[4096,2048]{1,0:T(8,128)(2,1)} %kernel_ref.1, bf16[4096,256]{1,0:T(8,128)(2,1)S(1)} %copy-done), kind=kOutput, calls=%fused_computation | convolution fusion | flops 4295491584 | bytes 19922944 | tf_op jit(solution)/shard_map/dot_general | solution.py:258
  10.1 20.5 %all_to_all.25 = bf16[8,256,256]{2,1,0:T(8,128)(2,1)S(1)} all-to-all(bf16[8,256,256]{2,1,0:T(8,128)(2,1)S(1)} %bitcast.15), channel_id=1, replica_groups=mesh['row'=8,'col'=16] {'row'}, dimensions={0} | all-to-all | bytes 2097152 | tf_op jit(solution)/shard_map/all_to_all | solution.py:256
  30.6 0.0 copy-start.2
  30.6 0.1 reduce_sum.12
  30.7 1.0 broadcast_in_dim.21
  31.8 4.5 %all-to-all-start.1 = ((bf16[8,256,256]{2,1,0:T(8,128)(2,1)}), bf16[8,256,256]{2,1,0:T(8,128)(2,1)S(1)}, u32[]{:S(2)}, u32[]{:S(2)}) async-start(bf16[8,256,256]{2,1,0:T(8,128)(2,1)} %broadcast_in_dim.21), calls=%async_computation.1 | async-start | bytes 2097152 | tf_op jit(solution)/shard_map/all_to_all | solution.py:256
  36.3 0.0 copy-done.2
  36.3 0.7 reshape.28.tree_ref
  37.0 14.3 %all-to-all-done.1 = bf16[8,256,256]{2,1,0:T(8,128)(2,1)S(1)} async-done(((bf16[8,256,256]{2,1,0:T(8,128)(2,1)}), bf16[8,256,256]{2,1,0:T(8,128)(2,1)S(1)}, u32[]{:S(2)}, u32[]{:S(2)}) %all-to-all-start.1) | async-done | bytes 1048608 | tf_op jit(solution)/shard_map/all_to_all | solution.py:256
  51.3 0.0 copy-start.1
  51.3 1.0 copy-done.1
  52.3 18.9 %second_pass.1 = bf16[2048,512]{1,0:T(8,128)(2,1)} custom-call(s32[1]{0:T(128)} %bitcast.1.first_ref, bf16[4096,2048]{1,0:T(8,128)(2,1)} %kernel_ref.1, bf16[2048,256]{1,0:T(8,128)(2,1)} %bitcast.13, s32[128,256]{1,0:T(8,128)} %reshape.28.tree_ref), custom_call_target="tpu_custom_call" | custom-call | tf_op jit(solution)/shard_map/second_pass/pallas_call | solution.py:268
  71.2 9.5 %all-to-all-start.2 = ((bf16[128,16,512]{2,1,0:T(8,128)(2,1)}), bf16[128,16,512]{2,1,0:T(8,128)(2,1)}, u32[]{:S(2)}, u32[]{:S(2)}) async-start(bf16[128,16,512]{2,1,0:T(8,128)(2,1)} %bitcast.11), calls=%async_computation.2 | async-start | bytes 4194304 | tf_op jit(solution)/shard_map/all_to_all | solution.py:256
  80.7 0.1 dynamic_slice.3
  80.8 28.8 %all-to-all-done.2 = bf16[128,16,512]{2,1,0:T(8,128)(2,1)} async-done(((bf16[128,16,512]{2,1,0:T(8,128)(2,1)}), bf16[128,16,512]{2,1,0:T(8,128)(2,1)}, u32[]{:S(2)}, u32[]{:S(2)}) %all-to-all-start.2) | async-done | bytes 2097184 | tf_op jit(solution)/shard_map/all_to_all | solution.py:256
  109.7 0.8 broadcast_in_dim.9.wanted_ref
  110.4 3.2 %collect.1 = (bf16[256,256]{1,0:T(8,128)(2,1)}, f32[1024,128]{1,0:T(8,128)}) custom-call(s32[256,128]{1,0:T(8,128)} %broadcast_in_dim.9.wanted_ref, bf16[8,16,16,512]{3,2,1,0:T(8,128)(2,1)} %bitcast.5.parts_ref), custom_call_target="tpu_custom_call" | custom-call | tf_op jit(solution)/shard_map/collect/pallas_call | solution.py:288
  113.6 20.1 %all_to_all.26 = f32[128,8,128]{2,1,0:T(8,128)} all-to-all(f32[128,8,128]{2,1,0:T(8,128)} %bitcast.16), channel_id=1, replica_groups=mesh['row'=8,'col'=16] {'row','col'}, dimensions={0} | all-to-all | bytes 1048576 | tf_op jit(solution)/shard_map/all_to_all | solution.py:256
  133.8 5.3 %node_sums.1 = f32[128,24,128]{2,1,0:T(8,128)} custom-call(s32[32]{0:T(128)} %units_ref.3, f32[1024,128]{1,0:T(8,128)} %bitcast.14), custom_call_target="tpu_custom_call" | custom-call | tf_op jit(solution)/shard_map/node_sums/pallas_call | solution.py:300
  139.0 29.1 %all_to_all.27 = f32[128,24,128]{2,1,0:T(8,128)} all-to-all(f32[128,24,128]{2,1,0:T(8,128)} %node_sums.1), channel_id=1, replica_groups=mesh['row'=8,'col'=16] {'row','col'}, dimensions={0} | all-to-all | bytes 3145728 | tf_op jit(solution)/shard_map/all_to_all | solution.py:256
  168.1 78.3 %node_bases.1 = bf16[4,256,256]{2,1,0:T(8,128)(2,1)} custom-call(s32[1]{0:T(128)} %bitcast.device_ref, s32[32]{0:T(128)} %units_ref.3, f32[3072,128]{1,0:T(8,128)} %bitcast.12, bf16[256,256]{1,0:T(8,128)(2,1)} %get-tuple-element.8.rows_ref), custom_call_target="tpu_custom_call" | custom-call | tf_op jit(solution)/shard_map/node_bases/pallas_call | solution.py:309
Async XLA Ops:
  0.0 1.6 copy-start
  30.6 5.7 %copy-start.2 = (s32[32768]{0:T(1024)S(1)}, s32[32768]{0:T(1024)}, u32[]{:S(2)}) copy-start(s32[32768]{0:T(1024)} %param.6) | copy-start | bytes 393220
  31.8 19.5 %all-to-all-start.1 = ((bf16[8,256,256]{2,1,0:T(8,128)(2,1)}), bf16[8,256,256]{2,1,0:T(8,128)(2,1)S(1)}, u32[]{:S(2)}, u32[]{:S(2)}) async-start(bf16[8,256,256]{2,1,0:T(8,128)(2,1)} %broadcast_in_dim.21), calls=%async_computation.1 | async-start | bytes 2097152 | tf_op jit(solution)/shard_map/all_to_all | solution.py:256
  51.3 1.0 copy-start.1
  71.2 38.5 %all-to-all-start.2 = ((bf16[128,16,512]{2,1,0:T(8,128)(2,1)}), bf16[128,16,512]{2,1,0:T(8,128)(2,1)}, u32[]{:S(2)}, u32[]{:S(2)}) async-start(bf16[128,16,512]{2,1,0:T(8,128)(2,1)} %bitcast.11), calls=%async_computation.2 | async-start | bytes 4194304 | tf_op jit(solution)/shard_map/all_to_all | solution.py:256

commit v2 on v1

v2 whole, which is shorter than its diff:
```python
import functools

import jax
import jax.numpy as jnp
from jax import lax
from jax.experimental import pallas as pl
from jax.experimental.pallas import tpu as pltpu
from jax.sharding import PartitionSpec as P

UNIT = 128
MINU = 4
LEVELS = 3
DEEP = 32
TOGETHER = 4
EACH = 2
BOTH = ("row", "col")
HIGHEST = lax.Precision.HIGHEST


def iota(shape, dim):
    return lax.broadcasted_iota(jnp.int32, shape, dim)


def choose(first_ref, tree_ref, out_ref, turned_ref):
    panel = out_ref.shape[0]
    rows, blocks = turned_ref.shape[1:]
    tree = jnp.transpose(tree_ref[...])
    turned_ref[0] = lax.shift_right_logical(tree, 8)
    turned_ref[1] = lax.bitwise_and(tree, rows - 1)
    place = iota((rows, blocks), 0)

    def one(step, carry):
        here = turned_ref[0] == first_ref[0] + step
        inner = turned_ref[1]
        low = jnp.min(jnp.where(here, inner, rows), axis=0, keepdims=True)
        high = jnp.max(jnp.where(here, inner, -1), axis=0, keepdims=True)
        for which, chosen in enumerate((low, high)):
            pick = jnp.transpose(jnp.where(place == chosen, 1.0, 0.0))
            out_ref[step, which * blocks : (which + 1) * blocks, :] = pick.astype(jnp.bfloat16)
        return carry

    lax.fori_loop(0, panel, one, 0)


def second_pass(kernel_ref, w_ref, pick_ref, out_ref, held_ref, ready_ref, spread_ref, sems):
    panel, blocks = pick_ref.shape[0], pick_ref.shape[1] // 2
    steps, tall, _ = held_ref.shape
    rows = pick_ref.shape[2]
    each = tall // rows

    def fetch(index):
        return pltpu.make_async_copy(
            kernel_ref.at[pl.ds(index * tall, tall), :], held_ref.at[index], sems.at[index]
        )

    def product(index):
        return jnp.dot(
            held_ref[index], w_ref[...], preferred_element_type=jnp.float32
        ).astype(jnp.bfloat16)

    def move(index):
        for inner in range(each):
            moved = jnp.dot(
                pick_ref[index * each + inner],
                ready_ref[inner * rows : (inner + 1) * rows, :],
                preferred_element_type=jnp.float32,
            )
            for column in range(spread_ref.shape[0]):
                which, half = column // 2, column % 2
                place = pl.ds(index * each + inner, blocks, stride=panel + 1)
                spread_ref[column, place, :] = moved[
                    which * blocks : (which + 1) * blocks, half * 128 : (half + 1) * 128
                ]

    for index in range(steps):
        fetch(index).start()
    fetch(0).wait()
    ready_ref[...] = product(0)

    def some(step, carry):
        fetch(step).wait()
        move(step - 1)
        ready_ref[...] = product(step)
        return carry

    lax.fori_loop(1, steps, some, 0)
    move(steps - 1)
    for column in range(spread_ref.shape[0]):
        for block in range(blocks):
            start = block * (panel + 1)
            out_ref[block * panel : (block + 1) * panel, column * 128 : (column + 1) * 128] = (
                spread_ref[column, start : start + panel, :].astype(jnp.bfloat16)
            )


def collect(wanted_ref, parts_ref, rows_ref, gram_ref):
    row_devices, col_devices, _, wide = parts_ref.shape
    width = wide // 2
    groups = []
    for row in range(row_devices):
        total = parts_ref[row, 0].astype(jnp.float32)
        for col in range(1, col_devices):
            total = total + parts_ref[row, col].astype(jnp.float32)
        groups.append(total)
    sample = jnp.concatenate(groups, axis=0).astype(jnp.bfloat16)
    blocks = sample.shape[0]
    wanted = wanted_ref[...]
    rows = wanted.shape[0]
    block = lax.shift_right_logical(wanted, 8)
    inside = lax.bitwise_and(wanted, rows - 1)
    same = block == iota((rows, blocks), 1)
    low = jnp.min(jnp.where(same, inside, rows), axis=0, keepdims=True)
    high = jnp.max(jnp.where(same, inside, -1), axis=0, keepdims=True)
    ordered = jnp.zeros((rows, width), jnp.float32)
    for which, chosen in enumerate((low, high)):
        pick = jnp.where(same & (inside == chosen), 1.0, 0.0).astype(jnp.bfloat16)
        ordered = ordered + jnp.dot(
            pick,
            sample[:, which * width : (which + 1) * width],
            preferred_element_type=jnp.float32,
        )
    ordered = ordered.astype(jnp.bfloat16)
    rows_ref[...] = ordered
    half = width // 2
    down, across = iota((half, half), 0), iota((half, half), 1)
    for unit in range(rows // UNIT):
        piece = ordered[unit * UNIT : (unit + 1) * UNIT]
        left, right = piece[:, :half], piece[:, half:]
        top, side, corner = [
            lax.dot_general(
                one, two, (((0,), (0,)), ((), ())), preferred_element_type=jnp.float32
            )
            for one, two in ((left, left), (right, left), (right, right))
        ]
        diagonal = jnp.sum(jnp.where(across == down, corner, 0.0), axis=0, keepdims=True)
        blocks_of = (
            jnp.where(across <= down, top, corner),
            side,
            jnp.broadcast_to(diagonal, (half, half)),
            jnp.zeros((half, half), jnp.float32),
        )
        for index, values in enumerate(blocks_of):
            gram_ref[pl.ds(unit * 4 + index, half, stride=8), :] = values


def leaf_of_unit(units_ref, unit):
    leaf = jnp.zeros_like(unit)
    end = jnp.int32(0)
    for index in range(units_ref.shape[0]):
        end = end + units_ref[index] + (MINU - 1)
        leaf = leaf + (unit >= end).astype(jnp.int32)
    return leaf


def exact_sum(member, values):
    total = jnp.zeros((member.shape[0], values.shape[1]), jnp.float32)
    for _ in range(3):
        piece = values.astype(jnp.bfloat16)
        values = values - piece.astype(jnp.float32)
        total = total + jnp.dot(member, piece, preferred_element_type=jnp.float32)
    return total


def node_sums(device_ref, units_ref, parts_ref, out_ref, diagonal_ref):
    devices = parts_ref.shape[0] // 8
    lanes = iota((8, devices), 1)
    row_leaf = [leaf_of_unit(units_ref, 2 * lanes + place)[0:1] for place in range(2)]
    row_leaf = jnp.concatenate(row_leaf, axis=1)
    wide = jnp.broadcast_to(row_leaf, (devices, 2 * devices))
    column_leaf = [
        jnp.transpose(wide[:, place * devices : (place + 1) * devices].astype(jnp.float32))
        for place in range(2)
    ]
    column_leaf = jnp.concatenate(column_leaf, axis=0).astype(jnp.int32)
    column_leaf = jnp.concatenate([column_leaf, column_leaf], axis=1)
    row_leaf = jnp.broadcast_to(row_leaf, column_leaf.shape)
    values = []
    for index in range(3):
        pieces = [
            parts_ref[pl.ds(place * 4 + index, devices, stride=8), :] for place in range(2)
        ]
        values.append(jnp.concatenate(pieces, axis=0))
    both = jnp.concatenate(values[:2], axis=1)
    slots = 2 * (LEVELS + 1)
    width = values[0].shape[1]
    for level in range(LEVELS + 1):
        match = lax.shift_right_logical(row_leaf, level) == lax.shift_right_logical(
            column_leaf, level
        )
        total = exact_sum(jnp.where(match, 1.0, 0.0).astype(jnp.bfloat16), both)
        for place in range(2):
            for index in range(2):
                out_ref[pl.ds(index * slots + 2 * level + place, devices, stride=2 * slots), :] = (
                    total[
                        place * devices : (place + 1) * devices,
                        index * width : (index + 1) * width,
                    ]
                )
    slot = iota((slots, 2 * devices), 0)
    level = lax.shift_right_logical(slot, 1)
    own = leaf_of_unit(units_ref, 2 * device_ref[0] + lax.bitwise_and(slot, 1))
    match = lax.shift_right_logical(row_leaf[:slots], level) == lax.shift_right_logical(own, level)
    diagonal_ref[...] = exact_sum(jnp.where(match, 1.0, 0.0).astype(jnp.bfloat16), values[2])


def spread_row(values, row):
    return jnp.broadcast_to(values[row : row + 1], values.shape)


def eliminate(group, base, lane, sub):
    inside = (lane >= base) & (lane < base + 8)
    eye = jnp.where(lane - base == sub, 1.0, 0.0)
    columns = [
        [jnp.broadcast_to(rows[:, base + i : base + i + 1], sub.shape) for i in range(8)]
        for rows in group
    ]
    values = [jnp.where(inside, eye, rows) for rows in group]
    scales = [jnp.zeros(sub.shape, jnp.float32) for _ in group]
    members = range(len(group))
    for i in range(8):
        roots = [lax.rsqrt(spread_row(columns[m][i], i)) for m in members]
        scales = [jnp.where(sub == i, roots[m], scales[m]) for m in members]
        if i < 7:
            below = [
                jnp.where(sub > i, columns[m][i] * (roots[m] * roots[m]), 0.0) for m in members
            ]
            for k in range(i + 1, 8):
                for m in members:
                    columns[m][k] = columns[m][k] - below[m] * spread_row(columns[m][k], i)
            values = [values[m] - below[m] * spread_row(values[m], i) for m in members]
    squares = [scale * scale for scale in scales]
    solved = [values[m] * squares[m] for m in members]
    for i in range(7, 0, -1):
        above = [jnp.where(sub < i, columns[m][i] * squares[m], 0.0) for m in members]
        solved = [solved[m] - above[m] * spread_row(solved[m], i) for m in members]
    return [values[m] * scales[m] for m in members], solved


def invert_factors(work_ref, panel_ref):
    count, size, lanes = work_ref.shape
    deep = panel_ref.shape[1]
    lane = iota((8, lanes), 1)
    sub = iota((8, lanes), 0)
    for start in range(0, size, deep):
        end = start + deep
        for base in range(start, end, 8):
            inside = (lane >= base) & (lane < base + 8)
            in_panel = (lane >= start) & (lane < end)
            done = {}
            for first in range(0, count, TOGETHER):
                batch = range(first, first + TOGETHER)
                pair = eliminate(
                    [work_ref[which, base : base + 8, :] for which in batch], base, lane, sub
                )
                for index, which in enumerate(batch):
                    done[which] = pair[0][index], pair[1][index]
            for which in range(count):
                scaled, solved = done[which]
                lower = lane <= base + sub
                if end < size:
                    panel_ref[which, base - start : base - start + 8, :] = jnp.where(
                        in_panel & (lane > base + sub), 0.0, scaled
                    )
                work_ref[which, base : base + 8, :] = jnp.where(lower, scaled, 0.0)
                for other in range(base + 8, end, 8):
                    rows = work_ref[which, other : other + 8, :]
                    total = jnp.where(inside, 0.0, rows)
                    for i in range(8):
                        column = jnp.broadcast_to(
                            rows[:, base + i : base + i + 1], rows.shape
                        )
                        total = total - column * spread_row(solved, i)
                    work_ref[which, other : other + 8, :] = total
        if end < size:
            wide = iota((deep, lanes), 1)
            rest = iota((size - end, lanes), 1)
            for which in range(count):
                panel = panel_ref[which]
                rows = work_ref[which, end:, :]
                factor = jnp.where((wide >= start) & (wide < end), panel, 0.0)
                part = dot_t(rows, factor)
                work_ref[which, end:, :] = jnp.where(
                    (rest >= start) & (rest < end), 0.0, rows
                ) - jnp.dot(
                    part, panel, precision=HIGHEST, preferred_element_type=jnp.float32
                )


def dot_t(one, two, precision=HIGHEST):
    return lax.dot_general(
        one,
        two,
        (((1,), (1,)), ((), ())),
        precision=precision,
        preferred_element_type=jnp.float32,
    )


def node_bases(
    device_ref,
    units_ref,
    node_ref,
    diagonal_ref,
    rows_ref,
    out_ref,
    work_ref,
    side_ref,
    last_ref,
    panel_ref,
):
    slots = work_ref.shape[0]
    half = work_ref.shape[1]
    stride = 2 * slots
    scales = []
    for slot in range(slots):
        level, unit = slot // 2, 2 * device_ref[0] + slot % 2
        leaf = jnp.int32(0)
        end = jnp.int32(0)
        for index in range(units_ref.shape[0]):
            end = end + units_ref[index] + (MINU - 1)
            leaf = leaf + (unit >= end).astype(jnp.int32)
        node = lax.shift_right_logical(leaf, level)
        count = jnp.int32(0)
        for index in range(units_ref.shape[0]):
            size = units_ref[index] + (MINU - 1)
            count = count + jnp.where(node == index >> level, size, 0)
        size = jnp.full((half, half), count * UNIT, jnp.int32).astype(jnp.float32)
        scales.append(size)
    down, across = iota((half, half), 0), iota((half, half), 1)
    for slot in range(slots):
        corners = node_ref[pl.ds(slot, half, stride=stride), :] / scales[slot]
        turned = jnp.transpose(corners)
        diagonal = jnp.broadcast_to(diagonal_ref[slot : slot + 1, :], (half, half))
        work_ref[slot] = jnp.where(across <= down, corners, turned)
        last_ref[slot] = jnp.where(
            across > down,
            corners,
            jnp.where(across == down, diagonal / scales[slot], turned),
        )
    invert_factors(work_ref, panel_ref)
    for slot in range(slots):
        below = node_ref[pl.ds(slots + slot, half, stride=stride), :] / scales[slot]
        side = dot_t(below, work_ref[slot])
        side_ref[slot] = side
        last_ref[slot] = last_ref[slot] - dot_t(side, side)
    invert_factors(last_ref, panel_ref)
    for slot in range(slots):
        level, unit = slot // 2, slot % 2
        piece = rows_ref[unit * UNIT : (unit + 1) * UNIT, :].astype(jnp.float32)
        first = dot_t(piece[:, :half], work_ref[slot])
        rest = piece[:, half:] - dot_t(first, side_ref[slot])
        second = dot_t(rest, last_ref[slot])
        place = slice(unit * UNIT, (unit + 1) * UNIT)
        out_ref[level, place, :half] = first.astype(jnp.bfloat16)
        out_ref[level, place, half:] = second.astype(jnp.bfloat16)


def shards(kernel, random_cols, tree_perm, leaf_units):
    f32, bf16 = jnp.float32, jnp.bfloat16
    width = random_cols.shape[1]
    half = width // 2
    row_devices, col_devices = lax.axis_size("row"), lax.axis_size("col")
    devices = row_devices * col_devices
    total_rows = tree_perm.shape[0]
    rows_dev = total_rows // devices
    panel = kernel.shape[0] // rows_dev
    slots = 2 * (LEVELS + 1)
    row = lax.axis_index("row")
    device = row * col_devices + lax.axis_index("col")
    vmem = pl.BlockSpec(memory_space=pltpu.VMEM)
    smem = pl.BlockSpec(memory_space=pltpu.SMEM)

    def exchange(values, axes):
        return lax.all_to_all(values, axes, 0, 0, tiled=True)

    partial_w = lax.dot_general(
        kernel, random_cols, (((0,), (0,)), ((), ())), preferred_element_type=f32
    ).astype(bf16)
    chunk = kernel.shape[1] // row_devices
    arrived = exchange(partial_w.reshape(row_devices, chunk, width), "row")
    own_w = jnp.sum(arrived.astype(f32), axis=0).astype(bf16)
    sample_w = exchange(jnp.broadcast_to(own_w[None], (row_devices, chunk, width)), "row")
    sample_w = sample_w.reshape(kernel.shape[1], width)

    tree = tree_perm.reshape(devices, rows_dev)
    hbm = pl.BlockSpec(memory_space=pl.ANY)
    picks = pl.pallas_call(
        choose,
        in_specs=[smem, vmem],
        out_specs=vmem,
        scratch_shapes=[pltpu.VMEM((2, rows_dev, devices), jnp.int32)],
        out_shape=jax.ShapeDtypeStruct((panel, 2 * devices, rows_dev), bf16),
        cost_estimate=pl.CostEstimate(
            flops=1 << 30, bytes_accessed=4 * devices * panel * rows_dev, transcendentals=0
        ),
        name="choose",
    )((row * panel)[None], tree)
    parts = pl.pallas_call(
        second_pass,
        in_specs=[hbm, vmem, vmem],
        out_specs=vmem,
        scratch_shapes=[
            pltpu.VMEM((panel // EACH, EACH * rows_dev, kernel.shape[1]), bf16),
            pltpu.VMEM((EACH * rows_dev, width), bf16),
            pltpu.VMEM((4, devices * (panel + 1), 128), f32),
            pltpu.SemaphoreType.DMA((panel // EACH,)),
        ],
        out_shape=jax.ShapeDtypeStruct((devices * panel, 2 * width), bf16),
        name="second_pass",
    )(kernel, sample_w, picks)
    parts = exchange(parts.reshape(devices, panel, 2 * width), BOTH)
    parts = parts.reshape(row_devices, col_devices, panel, 2 * width)

    wanted = lax.dynamic_slice_in_dim(tree_perm, device * rows_dev, rows_dev)
    wanted = jnp.broadcast_to(wanted[:, None], (rows_dev, devices))
    tree_rows, grams = pl.pallas_call(
        collect,
        in_specs=[vmem, vmem],
        out_specs=[vmem, vmem],
        out_shape=[
            jax.ShapeDtypeStruct((rows_dev, width), bf16),
            jax.ShapeDtypeStruct((devices * 8, half), f32),
        ],
        name="collect",
    )(wanted, parts)

    grams = exchange(grams.reshape(devices, 8, half), BOTH)
    nodes, diagonals = pl.pallas_call(
        node_sums,
        in_specs=[smem, smem, vmem],
        out_specs=[vmem, vmem],
        out_shape=[
            jax.ShapeDtypeStruct((devices * 2 * slots, half), f32),
            jax.ShapeDtypeStruct((slots, half), f32),
        ],
        name="node_sums",
    )(device[None], leaf_units, grams.reshape(devices * 8, half))
    nodes = exchange(nodes.reshape(devices, 2 * slots, half), BOTH)

    return pl.pallas_call(
        node_bases,
        in_specs=[smem, smem, vmem, vmem, vmem],
        out_specs=vmem,
        out_shape=jax.ShapeDtypeStruct((LEVELS + 1, rows_dev, width), bf16),
        scratch_shapes=[pltpu.VMEM((slots, half, half), f32)] * 3
        + [pltpu.VMEM((slots, DEEP, half), f32)],
        name="node_bases",
    )(device[None], leaf_units, nodes.reshape(devices * 2 * slots, half), diagonals, tree_rows)


def solution(mesh):
    return jax.shard_map(
        shards,
        mesh=mesh,
        in_specs=(P("row", "col"), P("row", None), P(), P()),
        out_specs=P(None, ("row", "col"), None),
        check_vma=False,
    )
```

time: 247 us -> 181 us (0.73)
  Pallas kernels: 106 us -> 49.4 us
  blocking collectives: 69.7 us -> 64.6 us
  waiting for transfers between devices: 43.1 us -> 38.2 us
    pallas_call x3 -> x4, Pallas kernels: 103 us -> 46.1 us  [the longest x1 26.5 us: shards(): pl.pallas_call(node_bases, in_specs=[smem, smem, vmem, vmem, vmem], out_s...]
    all_to_all x3, blocking collectives: 69.7 us -> 64.6 us  [exchange(): return lax.all_to_all(values, axes, 0, 0, tiled=True)]
    all_to_all x2, waiting for transfers between devices: 43.1 us -> 38.2 us  [exchange(): return lax.all_to_all(values, axes, 0, 0, tiled=True)]
  transfers between devices with their start and end apart: 2 -> 2, of which waited for: 2 -> 2; matrix products, arithmetic and copies ran while one was open for 0% -> 0% of each run, Pallas kernels for 0% -> 3%
where the time goes in v2:
time: 181 us; the launch traced here: 180 us
  blocking collectives  64.6 us (36%)
  Pallas kernels  49.4 us (27%)
  waiting for transfers between devices  38.2 us (21%)
  starting transfers between devices  14.1 us (8%)
  matrix products  8.46 us (5%)
  local copies, waits for them, and re-layouts  5.15 us (3%)
    all_to_all x3, blocking collectives, exchange(): return lax.all_to_all(values, axes, 0, 0, tiled=True)  64.6 us
    all_to_all x2, waiting for transfers between devices, exchange(): return lax.all_to_all(values, axes, 0, 0, tiled=True)  38.2 us
    pallas_call x1, Pallas kernels, shards(): pl.pallas_call(node_bases, in_specs=[smem, smem, vmem, vmem, vmem], out_s...  26.5 us
    all_to_all x2, starting transfers between devices, exchange(): return lax.all_to_all(values, axes, 0, 0, tiled=True)  14.1 us
    pallas_call x1, Pallas kernels, shards(): pl.pallas_call(second_pass, in_specs=[hbm, vmem, vmem], out_specs=vmem, s...  11.7 us
    dot_general x1, matrix products, shards(): lax.dot_general(kernel, random_cols, (((0,), (0,)), ((), ())), preferred_...  8.46 us
    pallas_call x1, Pallas kernels, shards(): pl.pallas_call(choose, in_specs=[smem, vmem], out_specs=vmem, scratch_sha...  4.92 us
  transfers between devices with their start and end apart: 2, of which 2 were waited for; matrix products, arithmetic and copies ran while one was open for 0% of the time, Pallas kernels for 3%

profile of v2, /device:TPU:1, one launch (start us, length us, event | category | flops | bytes accessed | tf_op | source)
XLA Modules:
  0.0 180.1 jit_solution(6210276905274681701)
XLA Ops:
  0.0 0.0 copy-start
  0.0 1.6 copy-done
  1.6 8.5 %convolution_convert_fusion = bf16[2048,256]{1,0:T(8,128)(2,1)S(1)} fusion(bf16[4096,2048]{1,0:T(8,128)(2,1)} %kernel_ref.1, bf16[4096,256]{1,0:T(8,128)(2,1)S(1)} %copy-done), kind=kOutput, calls=%fused_computation | convolution fusion | flops 4295491584 | bytes 19922944 | tf_op jit(solution)/shard_map/dot_general | solution.py:376
  10.1 20.5 %all_to_all.25 = bf16[8,256,256]{2,1,0:T(8,128)(2,1)S(1)} all-to-all(bf16[8,256,256]{2,1,0:T(8,128)(2,1)S(1)} %bitcast.17), channel_id=1, replica_groups=mesh['row'=8,'col'=16] {'row'}, dimensions={0} | all-to-all | bytes 2097152 | tf_op jit(solution)/shard_map/all_to_all | solution.py:374
  30.6 0.0 copy-start.2
  30.6 0.1 reduce_sum.12
  30.7 1.1 broadcast_in_dim.10
  31.8 4.5 %all-to-all-start.1 = ((bf16[8,256,256]{2,1,0:T(8,128)(2,1)}), bf16[8,256,256]{2,1,0:T(8,128)(2,1)S(1)}, u32[]{:S(2)}, u32[]{:S(2)}) async-start(bf16[8,256,256]{2,1,0:T(8,128)(2,1)} %broadcast_in_dim.10), calls=%async_computation.1 | async-start | bytes 2097152 | tf_op jit(solution)/shard_map/all_to_all | solution.py:374
  36.3 0.0 copy-done.2
  36.3 0.7 reshape.31.tree_ref
  37.0 4.9 %choose.1.pick_ref = bf16[16,256,256]{2,1,0:T(8,128)(2,1)} custom-call(s32[1]{0:T(128)} %bitcast.3.first_ref, s32[128,256]{1,0:T(8,128)} %reshape.31.tree_ref), custom_call_target="tpu_custom_call" | custom-call | flops 1073741824 | bytes 2097152 | tf_op jit(solution)/shard_map/choose/pallas_call | solution.py:387
  41.9 9.4 %all-to-all-done.1 = bf16[8,256,256]{2,1,0:T(8,128)(2,1)S(1)} async-done(((bf16[8,256,256]{2,1,0:T(8,128)(2,1)}), bf16[8,256,256]{2,1,0:T(8,128)(2,1)S(1)}, u32[]{:S(2)}, u32[]{:S(2)}) %all-to-all-start.1) | async-done | bytes 1048608 | tf_op jit(solution)/shard_map/all_to_all | solution.py:374
  51.3 0.0 copy-start.1
  51.3 1.0 copy-done.1
  52.3 11.7 %second_pass.1 = bf16[2048,512]{1,0:T(8,128)(2,1)} custom-call(bf16[4096,2048]{1,0:T(8,128)(2,1)} %kernel_ref.1, bf16[2048,256]{1,0:T(8,128)(2,1)} %bitcast.14, bf16[16,256,256]{2,1,0:T(8,128)(2,1)} %choose.1.pick_ref), custom_call_target="tpu_custom_call" | custom-call | tf_op jit(solution)/shard_map/second_pass/pallas_call | solution.py:398
  64.0 9.6 %all-to-all-start.2 = ((bf16[128,16,512]{2,1,0:T(8,128)(2,1)}), bf16[128,16,512]{2,1,0:T(8,128)(2,1)}, u32[]{:S(2)}, u32[]{:S(2)}) async-start(bf16[128,16,512]{2,1,0:T(8,128)(2,1)} %bitcast.12), calls=%async_computation.2 | async-start | bytes 4194304 | tf_op jit(solution)/shard_map/all_to_all | solution.py:374
  73.6 0.1 dynamic_slice.3
  73.7 28.8 %all-to-all-done.2 = bf16[128,16,512]{2,1,0:T(8,128)(2,1)} async-done(((bf16[128,16,512]{2,1,0:T(8,128)(2,1)}), bf16[128,16,512]{2,1,0:T(8,128)(2,1)}, u32[]{:S(2)}, u32[]{:S(2)}) %all-to-all-start.2) | async-done | bytes 2097184 | tf_op jit(solution)/shard_map/all_to_all | solution.py:374
  102.5 0.7 broadcast_in_dim.9.wanted_ref
  103.2 3.3 %collect.1 = (bf16[256,256]{1,0:T(8,128)(2,1)}, f32[1024,128]{1,0:T(8,128)}) custom-call(s32[256,128]{1,0:T(8,128)} %broadcast_in_dim.9.wanted_ref, bf16[8,16,16,512]{3,2,1,0:T(8,128)(2,1)} %bitcast.5.parts_ref), custom_call_target="tpu_custom_call" | custom-call | tf_op jit(solution)/shard_map/collect/pallas_call | solution.py:416
  106.5 20.1 %all_to_all.26 = f32[128,8,128]{2,1,0:T(8,128)} all-to-all(f32[128,8,128]{2,1,0:T(8,128)} %bitcast.18), channel_id=1, replica_groups=mesh['row'=8,'col'=16] {'row','col'}, dimensions={0} | all-to-all | bytes 1048576 | tf_op jit(solution)/shard_map/all_to_all | solution.py:374
  126.6 2.9 %node_sums.1 = (f32[2048,128]{1,0:T(8,128)}, f32[8,128]{1,0:T(8,128)}) custom-call(s32[1]{0:T(128)} %bitcast.device_ref, s32[32]{0:T(128)} %units_ref.3, f32[1024,128]{1,0:T(8,128)} %bitcast.15), custom_call_target="tpu_custom_call" | custom-call | tf_op jit(solution)/shard_map/node_sums/pallas_call | solution.py:428
  129.6 24.0 %all_to_all.27 = f32[128,16,128]{2,1,0:T(8,128)} all-to-all(f32[128,16,128]{2,1,0:T(8,128)} %bitcast.16), channel_id=1, replica_groups=mesh['row'=8,'col'=16] {'row','col'}, dimensions={0} | all-to-all | bytes 2097152 | tf_op jit(solution)/shard_map/all_to_all | solution.py:374
  153.6 26.5 %node_bases.1 = bf16[4,256,256]{2,1,0:T(8,128)(2,1)} custom-call(s32[1]{0:T(128)} %bitcast.device_ref, s32[32]{0:T(128)} %units_ref.3, f32[2048,128]{1,0:T(8,128)} %bitcast.13, f32[8,128]{1,0:T(8,128)} %get-tuple-element.11.diagonal_ref, bf16[256,256]{1,0:T(8,128)(2,1)} %get-tuple-element.12.rows_ref), custom_call_target="tpu_custom_call" | custom-call | tf_op jit(solution)/shard_map/node_bases/pallas_call | solution.py:440
Async XLA Ops:
  0.0 1.6 copy-start
  30.6 5.7 %copy-start.2 = (s32[32768]{0:T(1024)S(1)}, s32[32768]{0:T(1024)}, u32[]{:S(2)}) copy-start(s32[32768]{0:T(1024)} %param.6) | copy-start | bytes 393220
  31.8 19.5 %all-to-all-start.1 = ((bf16[8,256,256]{2,1,0:T(8,128)(2,1)}), bf16[8,256,256]{2,1,0:T(8,128)(2,1)S(1)}, u32[]{:S(2)}, u32[]{:S(2)}) async-start(bf16[8,256,256]{2,1,0:T(8,128)(2,1)} %broadcast_in_dim.10), calls=%async_computation.1 | async-start | bytes 2097152 | tf_op jit(solution)/shard_map/all_to_all | solution.py:374
  51.3 1.0 copy-start.1
  64.0 38.5 %all-to-all-start.2 = ((bf16[128,16,512]{2,1,0:T(8,128)(2,1)}), bf16[128,16,512]{2,1,0:T(8,128)(2,1)}, u32[]{:S(2)}, u32[]{:S(2)}) async-start(bf16[128,16,512]{2,1,0:T(8,128)(2,1)} %bitcast.12), calls=%async_computation.2 | async-start | bytes 4194304 | tf_op jit(solution)/shard_map/all_to_all | solution.py:374

commit v3 on v2

--- a/solution.py
+++ b/solution.py
@@ -21,12 +21,14 @@
     return lax.broadcasted_iota(jnp.int32, shape, dim)
 
 
-def choose(first_ref, tree_ref, out_ref, turned_ref):
+def choose(first_ref, tree_ref, out_ref, wanted_ref, turned_ref):
     panel = out_ref.shape[0]
     rows, blocks = turned_ref.shape[1:]
     tree = jnp.transpose(tree_ref[...])
     turned_ref[0] = lax.shift_right_logical(tree, 8)
     turned_ref[1] = lax.bitwise_and(tree, rows - 1)
+    own = tree_ref[pl.ds(first_ref[1], 1), :]
+    wanted_ref[...] = jnp.transpose(jnp.broadcast_to(own, (blocks, rows)))
     place = iota((rows, blocks), 0)
 
     def one(step, carry):
@@ -370,6 +372,9 @@
     vmem = pl.BlockSpec(memory_space=pltpu.VMEM)
     smem = pl.BlockSpec(memory_space=pltpu.SMEM)
 
+    def near(values):
+        return pltpu.with_memory_space_constraint(values, pltpu.VMEM)
+
     def exchange(values, axes):
         return lax.all_to_all(values, axes, 0, 0, tiled=True)
 
@@ -384,17 +389,20 @@
 
     tree = tree_perm.reshape(devices, rows_dev)
     hbm = pl.BlockSpec(memory_space=pl.ANY)
-    picks = pl.pallas_call(
+    picks, wanted = pl.pallas_call(
         choose,
         in_specs=[smem, vmem],
-        out_specs=vmem,
+        out_specs=[vmem, vmem],
         scratch_shapes=[pltpu.VMEM((2, rows_dev, devices), jnp.int32)],
-        out_shape=jax.ShapeDtypeStruct((panel, 2 * devices, rows_dev), bf16),
+        out_shape=[
+            jax.ShapeDtypeStruct((panel, 2 * devices, rows_dev), bf16),
+            jax.ShapeDtypeStruct((rows_dev, devices), jnp.int32),
+        ],
         cost_estimate=pl.CostEstimate(
             flops=1 << 30, bytes_accessed=4 * devices * panel * rows_dev, transcendentals=0
         ),
         name="choose",
-    )((row * panel)[None], tree)
+    )(jnp.stack([row * panel, device]), tree)
     parts = pl.pallas_call(
         second_pass,
         in_specs=[hbm, vmem, vmem],
@@ -407,22 +415,20 @@
         ],
         out_shape=jax.ShapeDtypeStruct((devices * panel, 2 * width), bf16),
         name="second_pass",
-    )(kernel, sample_w, picks)
+    )(kernel, near(sample_w), picks)
     parts = exchange(parts.reshape(devices, panel, 2 * width), BOTH)
     parts = parts.reshape(row_devices, col_devices, panel, 2 * width)
 
-    wanted = lax.dynamic_slice_in_dim(tree_perm, device * rows_dev, rows_dev)
-    wanted = jnp.broadcast_to(wanted[:, None], (rows_dev, devices))
     tree_rows, grams = pl.pallas_call(
         collect,
         in_specs=[vmem, vmem],
         out_specs=[vmem, vmem],
         out_shape=[
             jax.ShapeDtypeStruct((rows_dev, width), bf16),
-            jax.ShapeDtypeStruct((devices * 8, half), f32),
+            pltpu.VMEM((devices * 8, half), f32),
         ],
         name="collect",
-    )(wanted, parts)
+    )(wanted, near(parts))
 
     grams = exchange(grams.reshape(devices, 8, half), BOTH)
     nodes, diagonals = pl.pallas_call(
@@ -430,11 +436,11 @@
         in_specs=[smem, smem, vmem],
         out_specs=[vmem, vmem],
         out_shape=[
-            jax.ShapeDtypeStruct((devices * 2 * slots, half), f32),
+            pltpu.VMEM((devices * 2 * slots, half), f32),
             jax.ShapeDtypeStruct((slots, half), f32),
         ],
         name="node_sums",
-    )(device[None], leaf_units, grams.reshape(devices * 8, half))
+    )(device[None], leaf_units, near(grams.reshape(devices * 8, half)))
     nodes = exchange(nodes.reshape(devices, 2 * slots, half), BOTH)
 
     return pl.pallas_call(
@@ -445,7 +451,7 @@
         scratch_shapes=[pltpu.VMEM((slots, half, half), f32)] * 3
         + [pltpu.VMEM((slots, DEEP, half), f32)],
         name="node_bases",
-    )(device[None], leaf_units, nodes.reshape(devices * 2 * slots, half), diagonals, tree_rows)
+    )(device[None], leaf_units, near(nodes.reshape(devices * 2 * slots, half)), diagonals, tree_rows)
 
 
 def solution(mesh):

time: 181 us -> 175 us (0.967)
  blocking collectives: 64.6 us -> 100 us
  waiting for transfers between devices: 38.2 us -> 8.81 us
  starting transfers between devices: 14.1 us -> 4.5 us
  local copies, waits for them, and re-layouts: 5.15 us -> 1.76 us
  matrix products: 8.46 us -> 11.3 us
  Pallas kernels: 49.4 us -> 46.8 us
    all_to_all x3 -> x4, blocking collectives: 64.6 us -> 100 us  [exchange(): return lax.all_to_all(values, axes, 0, 0, tiled=True)]
    all_to_all x2 -> x1, waiting for transfers between devices: 38.2 us -> 8.81 us  [exchange(): return lax.all_to_all(values, axes, 0, 0, tiled=True)]
    all_to_all x2 -> x1, starting transfers between devices: 14.1 us -> 4.5 us  [exchange(): return lax.all_to_all(values, axes, 0, 0, tiled=True)]
    dot_general x1, matrix products: 8.46 us -> 11.3 us  [shards(): lax.dot_general(kernel, random_cols, (((0,), (0,)), ((), ())), preferred_...]
    unnamed x6 -> x2, local copies, waits for them, and re-layouts: 2.57 us -> 0.01 us
  transfers between devices with their start and end apart: 2 -> 1, of which waited for: 2 -> 1; matrix products, arithmetic and copies ran while one was open for 0% -> 1% of each run, Pallas kernels for 3% -> 3%
where the time goes in v3:
time: 175 us; the launch traced here: 174 us
  blocking collectives  100 us (57%)
  Pallas kernels  46.8 us (27%)
  matrix products  11.3 us (6%)
  waiting for transfers between devices  8.81 us (5%)
  starting transfers between devices  4.5 us (3%)
  local copies, waits for them, and re-layouts  1.76 us (1%)
    all_to_all x4, blocking collectives, exchange(): return lax.all_to_all(values, axes, 0, 0, tiled=True)  100 us
    pallas_call x1, Pallas kernels, shards(): pl.pallas_call(node_bases, in_specs=[smem, smem, vmem, vmem, vmem], out_s...  26.2 us
    pallas_call x1, Pallas kernels, shards(): pl.pallas_call(second_pass, in_specs=[hbm, vmem, vmem], out_specs=vmem, s...  11.4 us
    dot_general x1, matrix products, shards(): lax.dot_general(kernel, random_cols, (((0,), (0,)), ((), ())), preferred_...  11.3 us
    all_to_all x1, waiting for transfers between devices, exchange(): return lax.all_to_all(values, axes, 0, 0, tiled=True)  8.81 us
    pallas_call x1, Pallas kernels, shards(): pl.pallas_call(choose, in_specs=[smem, vmem], out_specs=[vmem, vmem], scr...  4.94 us
    all_to_all x1, starting transfers between devices, exchange(): return lax.all_to_all(values, axes, 0, 0, tiled=True)  4.5 us
  transfers between devices with their start and end apart: 1, of which 1 were waited for; matrix products, arithmetic and copies ran while one was open for 1% of the time, Pallas kernels for 3%

profile of v3, /device:TPU:1, one launch (start us, length us, event | category | flops | bytes accessed | tf_op | source)
XLA Modules:
  0.0 174.3 jit_solution(13758756986089872619)
XLA Ops:
  0.0 11.3 %convolution_convert_fusion = bf16[2048,256]{1,0:T(8,128)(2,1)S(1)} fusion(bf16[4096,2048]{1,0:T(8,128)(2,1)} %kernel_ref.1, bf16[4096,256]{1,0:T(8,128)(2,1)} %param.5), kind=kOutput, calls=%fused_computation | convolution fusion | flops 4295491584 | bytes 19922944 | tf_op jit(solution)/shard_map/dot_general | solution.py:381
  11.3 20.5 %all_to_all.25 = bf16[8,256,256]{2,1,0:T(8,128)(2,1)S(1)} all-to-all(bf16[8,256,256]{2,1,0:T(8,128)(2,1)S(1)} %bitcast.19), channel_id=1, replica_groups=mesh['row'=8,'col'=16] {'row'}, dimensions={0} | all-to-all | bytes 2097152 | tf_op jit(solution)/shard_map/all_to_all | solution.py:379
  31.8 0.0 copy-start
  31.8 0.1 reduce_sum.12
  32.0 1.1 broadcast_in_dim.5
  33.0 4.5 %all-to-all-start.1 = ((bf16[8,256,256]{2,1,0:T(8,128)(2,1)}), bf16[8,256,256]{2,1,0:T(8,128)(2,1)S(1)}, u32[]{:S(2)}, u32[]{:S(2)}) async-start(bf16[8,256,256]{2,1,0:T(8,128)(2,1)} %broadcast_in_dim.5), calls=%async_computation.1 | async-start | bytes 2097152 | tf_op jit(solution)/shard_map/all_to_all | solution.py:379
  37.5 0.0 copy-done
  37.6 0.7 reshape.28.tree_ref
  38.2 0.6 pad_add_fusion.first_ref
  38.8 4.9 %choose.1 = (bf16[16,256,256]{2,1,0:T(8,128)(2,1)}, s32[256,128]{1,0:T(8,128)}) custom-call(s32[2]{0:T(128)} %pad_add_fusion.first_ref, s32[128,256]{1,0:T(8,128)} %reshape.28.tree_ref), custom_call_target="tpu_custom_call" | custom-call | flops 1073741824 | bytes 2097152 | tf_op jit(solution)/shard_map/choose/pallas_call | solution.py:392
  43.7 8.8 %all-to-all-done.1 = bf16[8,256,256]{2,1,0:T(8,128)(2,1)S(1)} async-done(((bf16[8,256,256]{2,1,0:T(8,128)(2,1)}), bf16[8,256,256]{2,1,0:T(8,128)(2,1)S(1)}, u32[]{:S(2)}, u32[]{:S(2)}) %all-to-all-start.1) | async-done | bytes 1048608 | tf_op jit(solution)/shard_map/all_to_all | solution.py:379
  52.5 11.4 %second_pass.1 = bf16[2048,512]{1,0:T(8,128)(2,1)} custom-call(bf16[4096,2048]{1,0:T(8,128)(2,1)} %kernel_ref.1, bf16[2048,256]{1,0:T(8,128)(2,1)S(1)} %bitcast.14, bf16[16,256,256]{2,1,0:T(8,128)(2,1)} %get-tuple-element.12.pick_ref), custom_call_target="tpu_custom_call" | custom-call | tf_op jit(solution)/shard_map/second_pass/pallas_call | solution.py:406
  64.0 38.4 %all_to_all.26 = bf16[128,16,512]{2,1,0:T(8,128)(2,1)S(1)} all-to-all(bf16[128,16,512]{2,1,0:T(8,128)(2,1)} %bitcast.18), channel_id=1, replica_groups=mesh['row'=8,'col'=16] {'row','col'}, dimensions={0} | all-to-all | bytes 4194304 | tf_op jit(solution)/shard_map/all_to_all | solution.py:379
  102.3 2.1 %collect.1 = (bf16[256,256]{1,0:T(8,128)(2,1)}, f32[1024,128]{1,0:T(8,128)S(1)}) custom-call(s32[256,128]{1,0:T(8,128)} %get-tuple-element.11.wanted_ref, bf16[8,16,16,512]{3,2,1,0:T(8,128)(2,1)S(1)} %bitcast.12), custom_call_target="tpu_custom_call" | custom-call | tf_op jit(solution)/shard_map/collect/pallas_call | solution.py:422
  104.4 18.9 %all_to_all.27 = f32[128,8,128]{2,1,0:T(8,128)S(1)} all-to-all(f32[128,8,128]{2,1,0:T(8,128)S(1)} %bitcast.17), channel_id=1, replica_groups=mesh['row'=8,'col'=16] {'row','col'}, dimensions={0} | all-to-all | bytes 1048576 | tf_op jit(solution)/shard_map/all_to_all | solution.py:379
  123.3 2.1 %node_sums.1 = (f32[2048,128]{1,0:T(8,128)S(1)}, f32[8,128]{1,0:T(8,128)}) custom-call(s32[1]{0:T(128)} %bitcast.device_ref, s32[32]{0:T(128)} %units_ref.3, f32[1024,128]{1,0:T(8,128)S(1)} %bitcast.15), custom_call_target="tpu_custom_call" | custom-call | tf_op jit(solution)/shard_map/node_sums/pallas_call | solution.py:434
  125.4 22.7 %all_to_all.28 = f32[128,16,128]{2,1,0:T(8,128)S(1)} all-to-all(f32[128,16,128]{2,1,0:T(8,128)S(1)} %bitcast.16), channel_id=1, replica_groups=mesh['row'=8,'col'=16] {'row','col'}, dimensions={0} | all-to-all | bytes 2097152 | tf_op jit(solution)/shard_map/all_to_all | solution.py:379
  148.1 26.2 %node_bases.1 = bf16[4,256,256]{2,1,0:T(8,128)(2,1)} custom-call(s32[1]{0:T(128)} %bitcast.device_ref, s32[32]{0:T(128)} %units_ref.3, f32[2048,128]{1,0:T(8,128)S(1)} %bitcast.13, f32[8,128]{1,0:T(8,128)} %get-tuple-element.15.diagonal_ref, bf16[256,256]{1,0:T(8,128)(2,1)} %get-tuple-element.16.rows_ref), custom_call_target="tpu_custom_call" | custom-call | tf_op jit(solution)/shard_map/node_bases/pallas_call | solution.py:446
Async XLA Ops:
  31.8 5.7 %copy-start = (s32[32768]{0:T(1024)S(1)}, s32[32768]{0:T(1024)}, u32[]{:S(2)}) copy-start(s32[32768]{0:T(1024)} %param.6) | copy-start | bytes 393220
  33.0 19.5 %all-to-all-start.1 = ((bf16[8,256,256]{2,1,0:T(8,128)(2,1)}), bf16[8,256,256]{2,1,0:T(8,128)(2,1)S(1)}, u32[]{:S(2)}, u32[]{:S(2)}) async-start(bf16[8,256,256]{2,1,0:T(8,128)(2,1)} %broadcast_in_dim.5), calls=%async_computation.1 | async-start | bytes 2097152 | tf_op jit(solution)/shard_map/all_to_all | solution.py:379

commit v4 on v3

--- a/solution.py
+++ b/solution.py
@@ -416,6 +416,7 @@
         out_shape=jax.ShapeDtypeStruct((devices * panel, 2 * width), bf16),
         name="second_pass",
     )(kernel, near(sample_w), picks)
+    parts = parts * (leaf_units[0] > 0).astype(bf16)
     parts = exchange(parts.reshape(devices, panel, 2 * width), BOTH)
     parts = parts.reshape(row_devices, col_devices, panel, 2 * width)
 

time: 175 us -> 176 us (level)
  other arithmetic: 0.7 us -> 2.53 us
where the time goes in v4:
time: 176 us
  blocking collectives  100 us (57%)
  Pallas kernels  46.8 us (27%)
  matrix products  11.3 us (6%)
  waiting for transfers between devices  8.66 us (5%)
  starting transfers between devices  4.5 us (3%)
  other arithmetic  2.53 us (1%)
  local copies, waits for them, and re-layouts  1.76 us (1%)
    all_to_all x4, blocking collectives, exchange(): return lax.all_to_all(values, axes, 0, 0, tiled=True)  100 us
    pallas_call x1, Pallas kernels, shards(): pl.pallas_call(node_bases, in_specs=[smem, smem, vmem, vmem, vmem], out_s...  26.2 us
    pallas_call x1, Pallas kernels, shards(): pl.pallas_call(second_pass, in_specs=[hbm, vmem, vmem], out_specs=vmem, s...  11.4 us
    dot_general x1, matrix products, shards(): lax.dot_general(kernel, random_cols, (((0,), (0,)), ((), ())), preferred_...  11.3 us
    all_to_all x1, waiting for transfers between devices, exchange(): return lax.all_to_all(values, axes, 0, 0, tiled=True)  8.66 us
    pallas_call x1, Pallas kernels, shards(): pl.pallas_call(choose, in_specs=[smem, vmem], out_specs=[vmem, vmem], scr...  4.93 us
    all_to_all x1, starting transfers between devices, exchange(): return lax.all_to_all(values, axes, 0, 0, tiled=True)  4.5 us
  transfers between devices with their start and end apart: 1, of which 1 were waited for; matrix products, arithmetic and copies ran while one was open for 1% of the time, Pallas kernels for 3%

profile of v4, /device:TPU:1, one launch (start us, length us, event | category | flops | bytes accessed | tf_op | source)
XLA Modules:
  0.0 175.8 jit_solution(17481412785255668962)
XLA Ops:
  0.0 11.3 %convolution_convert_fusion = bf16[2048,256]{1,0:T(8,128)(2,1)S(1)} fusion(bf16[4096,2048]{1,0:T(8,128)(2,1)} %kernel_ref.1, bf16[4096,256]{1,0:T(8,128)(2,1)} %param.5), kind=kOutput, calls=%fused_computation | convolution fusion | flops 4295491584 | bytes 19922944 | tf_op jit(solution)/shard_map/dot_general | solution.py:381
  11.3 20.5 %all_to_all.25 = bf16[8,256,256]{2,1,0:T(8,128)(2,1)S(1)} all-to-all(bf16[8,256,256]{2,1,0:T(8,128)(2,1)S(1)} %bitcast.21), channel_id=1, replica_groups=mesh['row'=8,'col'=16] {'row'}, dimensions={0} | all-to-all | bytes 2097152 | tf_op jit(solution)/shard_map/all_to_all | solution.py:379
  31.8 0.0 copy-start
  31.8 0.0 copy-start.1
  31.8 0.1 reduce_sum.12
  32.0 1.1 broadcast_in_dim.5
  33.0 4.5 %all-to-all-start.1 = ((bf16[8,256,256]{2,1,0:T(8,128)(2,1)}), bf16[8,256,256]{2,1,0:T(8,128)(2,1)S(1)}, u32[]{:S(2)}, u32[]{:S(2)}) async-start(bf16[8,256,256]{2,1,0:T(8,128)(2,1)} %broadcast_in_dim.5), calls=%async_computation.1 | async-start | bytes 2097152 | tf_op jit(solution)/shard_map/all_to_all | solution.py:379
  37.5 0.0 copy-done
  37.5 0.7 reshape.32.tree_ref
  38.2 0.0 copy-done.1
  38.3 0.6 pad_add_fusion.first_ref
  38.9 4.9 %choose.1 = (bf16[16,256,256]{2,1,0:T(8,128)(2,1)}, s32[256,128]{1,0:T(8,128)}) custom-call(s32[2]{0:T(128)} %pad_add_fusion.first_ref, s32[128,256]{1,0:T(8,128)} %reshape.32.tree_ref), custom_call_target="tpu_custom_call" | custom-call | flops 1073741824 | bytes 2097152 | tf_op jit(solution)/shard_map/choose/pallas_call | solution.py:392
  43.9 8.7 %all-to-all-done.1 = bf16[8,256,256]{2,1,0:T(8,128)(2,1)S(1)} async-done(((bf16[8,256,256]{2,1,0:T(8,128)(2,1)}), bf16[8,256,256]{2,1,0:T(8,128)(2,1)S(1)}, u32[]{:S(2)}, u32[]{:S(2)}) %all-to-all-start.1) | async-done | bytes 1048608 | tf_op jit(solution)/shard_map/all_to_all | solution.py:379
  52.5 11.4 %second_pass.1 = bf16[2048,512]{1,0:T(8,128)(2,1)} custom-call(bf16[4096,2048]{1,0:T(8,128)(2,1)} %kernel_ref.1, bf16[2048,256]{1,0:T(8,128)(2,1)S(1)} %bitcast.16, bf16[16,256,256]{2,1,0:T(8,128)(2,1)} %get-tuple-element.12.pick_ref), custom_call_target="tpu_custom_call" | custom-call | tf_op jit(solution)/shard_map/second_pass/pallas_call | solution.py:406
  64.0 1.7 broadcast_multiply_fusion
  65.7 38.2 %all_to_all.26 = bf16[128,16,512]{2,1,0:T(8,128)(2,1)S(1)} all-to-all(bf16[128,16,512]{2,1,0:T(8,128)(2,1)S(1)} %bitcast.20), channel_id=1, replica_groups=mesh['row'=8,'col'=16] {'row','col'}, dimensions={0} | all-to-all | bytes 4194304 | tf_op jit(solution)/shard_map/all_to_all | solution.py:379
  103.9 2.1 %collect.1 = (bf16[256,256]{1,0:T(8,128)(2,1)}, f32[1024,128]{1,0:T(8,128)S(1)}) custom-call(s32[256,128]{1,0:T(8,128)} %get-tuple-element.11.wanted_ref, bf16[8,16,16,512]{3,2,1,0:T(8,128)(2,1)S(1)} %bitcast.14), custom_call_target="tpu_custom_call" | custom-call | tf_op jit(solution)/shard_map/collect/pallas_call | solution.py:423
  106.0 18.9 %all_to_all.27 = f32[128,8,128]{2,1,0:T(8,128)S(1)} all-to-all(f32[128,8,128]{2,1,0:T(8,128)S(1)} %bitcast.19), channel_id=1, replica_groups=mesh['row'=8,'col'=16] {'row','col'}, dimensions={0} | all-to-all | bytes 1048576 | tf_op jit(solution)/shard_map/all_to_all | solution.py:379
  124.8 2.1 %node_sums.1 = (f32[2048,128]{1,0:T(8,128)S(1)}, f32[8,128]{1,0:T(8,128)}) custom-call(s32[1]{0:T(128)} %bitcast.device_ref, s32[32]{0:T(128)} %units_ref.3, f32[1024,128]{1,0:T(8,128)S(1)} %bitcast.17), custom_call_target="tpu_custom_call" | custom-call | tf_op jit(solution)/shard_map/node_sums/pallas_call | solution.py:435
  126.9 22.7 %all_to_all.28 = f32[128,16,128]{2,1,0:T(8,128)S(1)} all-to-all(f32[128,16,128]{2,1,0:T(8,128)S(1)} %bitcast.18), channel_id=1, replica_groups=mesh['row'=8,'col'=16] {'row','col'}, dimensions={0} | all-to-all | bytes 2097152 | tf_op jit(solution)/shard_map/all_to_all | solution.py:379
  149.6 26.2 %node_bases.1 = bf16[4,256,256]{2,1,0:T(8,128)(2,1)} custom-call(s32[1]{0:T(128)} %bitcast.device_ref, s32[32]{0:T(128)} %units_ref.3, f32[2048,128]{1,0:T(8,128)S(1)} %bitcast.15, f32[8,128]{1,0:T(8,128)} %get-tuple-element.15.diagonal_ref, bf16[256,256]{1,0:T(8,128)(2,1)} %get-tuple-element.16.rows_ref), custom_call_target="tpu_custom_call" | custom-call | tf_op jit(solution)/shard_map/node_bases/pallas_call | solution.py:447
Async XLA Ops:
  31.8 5.7 %copy-start = (s32[32768]{0:T(1024)S(1)}, s32[32768]{0:T(1024)}, u32[]{:S(2)}) copy-start(s32[32768]{0:T(1024)} %param.6) | copy-start | bytes 393220
  31.8 6.4 %copy-start.1 = (s32[32]{0:T(128)S(1)}, s32[32]{0:T(128)}, u32[]{:S(2)}) copy-start(s32[32]{0:T(128)} %units_ref.3) | copy-start | bytes 388
  33.0 19.5 %all-to-all-start.1 = ((bf16[8,256,256]{2,1,0:T(8,128)(2,1)}), bf16[8,256,256]{2,1,0:T(8,128)(2,1)S(1)}, u32[]{:S(2)}, u32[]{:S(2)}) async-start(bf16[8,256,256]{2,1,0:T(8,128)(2,1)} %broadcast_in_dim.5), calls=%async_computation.1 | async-start | bytes 2097152 | tf_op jit(solution)/shard_map/all_to_all | solution.py:379
